TPU v7x, 128 devices: a whole 4x4x4 slice. The times are simulated.
128 devices in a mesh: trade: 16 (over y, x), path: 8 (over z, core).
Axes of the slice: x: 4, y: 4, z: 4, core: 2. Of those that a mesh axis runs over, the one named last changes fastest.
Arguments:
- deltas: bfloat16 [65536, 1024], P('trade', 'path'), may hold values from -0.0039978027 to 0.0039978027
- net_ids: int32 [65536], P('trade'), may hold values from 0 to 7, as said below
- block_ids: int32 [65536], P('trade'), may hold values from 0 to 13823
- bucket_map: int32 [13824], replicated, may hold values from 0 to 1151
- risk_weight: float32 [13824], replicated, may hold values from 10 to 80
- counts: int32 [16], P('trade'), may hold values from 1 to 4096, 39321 in all
- correlation: float32 [1152, 1152], replicated, may hold values from -1 to 3, as said below
- path_weight: float32 [1024], P('path'), may hold values from 0.2 to 16.2, as said below
- margin_cotangent: float32 [8, 1024], P(None, 'path'), may hold values from -6 to 6
Outputs:
- margin: float32 [8, 1024], P(None, 'path')
- expected: float32 [8], replicated
- trade_grad: bfloat16 [65536, 1024], P('trade', 'path')
Inputs may be any that keep to these rules, and one draw needn't show every extreme that they name: The live trades of group g fill its first counts[g] of 4096 slots; some group is full. `net_ids`: among the 4096 slots of one trade group each netting set appears at most 768 times, and in every group one netting set appears exactly 768 times. `correlation`: symmetric and positive definite. `path_weight`: Positive.
All inputs are finite; a program needn't handle non-finite values.
Results may differ from a plain program's by a relative error of at most 0.0054.
The roundings to bfloat16 on the way count: a program that leaves them out, or rounds other values in their place, can miss the bound.
Values may be sent and summed in bfloat16 or wider, within the bound.
A program may use at most 64 MiB of HBM per device.

v0:
```python
import jax
import jax.numpy as jnp
from jax import lax
from jax.sharding import PartitionSpec as P

EPSILON = 1e-06


def split_up(x, dim, size):
    lengths = x.shape
    tiles = x.reshape(*lengths[:dim], size, lengths[dim] // size, *lengths[dim + 1 :])
    return jnp.moveaxis(tiles, dim, 0)


def summed_on_arrival(x, axis, dim):
    tiles = split_up(x, dim, lax.axis_size(axis))
    arrived = lax.all_to_all(tiles, axis, split_axis=0, concat_axis=0, tiled=True)
    return arrived.astype(jnp.float32).sum(axis=0)


def laid_out(tiles, dim):
    tiles = jnp.moveaxis(tiles, 0, dim)
    lengths = tiles.shape
    return tiles.reshape(*lengths[:dim], lengths[dim] * lengths[dim + 1], *lengths[dim + 2 :])


def from_everyone(x, axis):
    size = lax.axis_size(axis)
    return lax.all_to_all(jnp.broadcast_to(x[None], (size, *x.shape)), axis, 0, 0, tiled=True)


def gather_directly(x, axis, dim):
    return laid_out(from_everyone(x, axis), dim)


def shards(
    deltas,
    net_ids,
    block_ids,
    bucket_map,
    risk_weight,
    counts,
    correlation,
    path_weight,
    margin_cotangent,
):
    capacity, path_count = deltas.shape
    bucket_count = correlation.shape[0]
    net_count = margin_cotangent.shape[0]
    columns = net_count * path_count
    groups = lax.axis_size("trade")
    trade_weight = risk_weight[block_ids]
    trade_bucket = bucket_map[block_ids]
    live_count = counts[0]
    is_live = jnp.arange(capacity, dtype=jnp.int32) < live_count
    weighted = jnp.where(
        is_live[:, None], trade_weight[:, None] * deltas.astype(jnp.float32), 0.0
    ).astype(jnp.bfloat16)
    block_len = min(512, capacity)
    live_blocks = (live_count + block_len - 1) // block_len
    shard_len = columns // groups
    own_start = lax.axis_index("trade") * shard_len
    own_cotangent = lax.dynamic_slice_in_dim(
        margin_cotangent.reshape(columns), own_start, shard_len
    )
    column_ids = jnp.arange(shard_len * lax.axis_size("trade"), dtype=jnp.int32)
    net_of = column_ids // path_count
    path_of = column_ids % path_count
    bucket_range = jnp.arange(bucket_count, dtype=jnp.int32)

    def add_block(partial_value, first_row):
        bucket_ids = lax.dynamic_slice_in_dim(trade_bucket, first_row, block_len)
        net_block = lax.dynamic_slice_in_dim(net_ids, first_row, block_len)
        row_block = lax.dynamic_slice_in_dim(weighted, first_row, block_len, 0)
        delta_rows = jnp.where(
            net_block[:, None] == net_of[None, :],
            row_block[:, path_of],
            jnp.zeros((), jnp.bfloat16),
        )
        bucket_hot = (bucket_ids[:, None] == bucket_range[None, :]).astype(jnp.bfloat16)
        return partial_value + jnp.einsum(
            "tc,tb->cb", delta_rows, bucket_hot, preferred_element_type=jnp.float32
        )

    def advance(block_number, partial_value):
        return add_block(partial_value, block_number * block_len)

    summed = summed_on_arrival(
        lax.fori_loop(
            0,
            live_blocks,
            advance,
            jnp.zeros((shard_len * lax.axis_size("trade"), bucket_count), jnp.float32),
        ).astype(jnp.bfloat16),
        "trade",
        0,
    )
    coupled = jnp.dot(
        summed, correlation, precision=lax.Precision.HIGHEST, preferred_element_type=jnp.float32
    )
    margin_part = jnp.sqrt(jnp.sum(summed * coupled, axis=1) + EPSILON)
    margin = gather_directly(margin_part, "trade", 0).reshape(net_count, path_count)
    bucket_grad = ((own_cotangent / margin_part)[:, None] * coupled).astype(jnp.bfloat16)
    all_hot = (trade_bucket[:, None] == jnp.arange(bucket_count, dtype=jnp.int32)[None, :]).astype(
        jnp.bfloat16
    )
    looked_up = jnp.einsum(
        "tb,cb->tc",
        all_hot,
        gather_directly(bucket_grad, "trade", 0),
        preferred_element_type=jnp.float32,
    )
    net_match = net_ids[:, None] == jnp.arange(net_count, dtype=jnp.int32)[None, :]
    chosen = jnp.sum(
        jnp.where(net_match[:, :, None], looked_up.reshape(capacity, net_count, path_count), 0.0),
        axis=1,
    )
    weighted_sum = jnp.sum(margin * path_weight[None, :], axis=1)
    expected = lax.psum(weighted_sum, "path") / (path_count * lax.axis_size("path"))
    trade_grad = jnp.where(is_live[:, None], trade_weight[:, None] * chosen, 0.0).astype(
        jnp.bfloat16
    )
    return (margin, expected, trade_grad)


def solution(mesh):
    placed = (
        P("trade", "path"),
        P("trade"),
        P("trade"),
        P(),
        P(),
        P("trade"),
        P(),
        P("path"),
        P(None, "path"),
    )
    return jax.shard_map(
        shards,
        mesh=mesh,
        in_specs=placed,
        out_specs=(P(None, "path"), P(), P("trade", "path")),
        check_vma=False,
    )
```

profile of v0, /device:TPU:0, one launch (start us, length us, event | category | flops | bytes accessed | tf_op | source)
XLA Modules:
  0.0 254.1 jit_solution(2610295243066201353)
XLA Ops:
  0.6 0.0 copy-start
  1.3 0.7 fusion.25
  2.0 0.0 copy-done
  2.1 0.0 copy-start.1
  2.1 23.0 %gather_fusion.1 = f32[4096]{0:T(1024)S(1)} fusion(f32[13824]{0:T(1024)S(1)} %copy-done, s32[4096]{0:T(1024)S(1)} %fusion.25), kind=kCustom, calls=%fused_computation.1 | custom fusion | bytes 49152 | tf_op jit(solution)/shard_map/gather | solution.py:52
  25.1 0.0 copy-done.1
  25.1 0.0 copy-start.2
  25.1 23.0 %gather_fusion.2 = s32[4096]{0:T(1024)S(1)} fusion(s32[13824]{0:T(1024)S(1)} %copy-done.1, s32[4096]{0:T(1024)S(1)} %fusion.25), kind=kCustom, calls=%fused_computation.2 | custom fusion | bytes 49152 | tf_op jit(solution)/shard_map/gather | solution.py:53
  48.2 0.0 copy-done.2
  48.2 1.4 select_convert_fusion.1
  49.6 0.0 copy-start.3
  49.6 2.4 broadcast_in_dim.41
  52.1 0.0 copy-done.3
  52.1 21.1 %while.11 = (s32[]{:T(128)}, f32[1024,1152]{1,0:T(8,128)}, s32[]{:T(128)}, s32[4096]{0:T(1024)S(1)}, bf16[4096,128]{1,0:T(8,128)(2,1)S(1)}, /*index=5*/s32[4096]...) while((s32[]{:T(128)}, f32[1024,1152]{1,0:T(8,128)}, s32[]{:T(128)}, s32[4096]{0:T(1024)S(1)}, ...), condition=%wide.region_1.2_spmd.clone, body=%wide.region_0.1_spmd.clone.sunk | while | flops 1210796032 | bytes 13152415 | solution.py:89
  52.1 0.1 copy.17
  52.2 4.0 %gather_fusion = bf16[1024,512]{1,0:T(8,128)(2,1)S(1)} fusion(bf16[512,128]{0,1:T(8,128)(2,1)S(1)} %copy.17, s32[1024]{0:T(1024)S(1)} %broadcast_clamp_fusion.2), kind=kCustom, calls=%fused_computation.clone.clone.1 | custom fusion | bytes 2101248 | tf_op jit(solution)/shard_map/while/body/gather | solution.py:77
  56.2 0.1 dynamic_slice.22
  56.3 0.1 dynamic_slice.23
  56.4 6.2 %convolution_add_fusion.2 = f32[1024,1152]{1,0:T(8,128)} fusion(f32[1024,1152]{1,0:T(8,128)} %get-tuple-element.152, s32[512]{0:T(512)S(1)} %dynamic_slice.22, bf16[1024,512]{1,0:T(8,128)(2,1)S(1)} %gather_fusion, s32[512]{0:T(512)S(1)} %dynamic_slice.23, s32[1024]{0:T(1024)S(1)} %add_select_fusion.2), kind=kOutput, calls=%fused_computation.6.clone.1 | convolution fusion | flops 1210777600 | bytes 10493952 | tf_op jit(solution)/shard_map/while/body/tc,tb->cb/dot_general | solution.py:81
  62.6 0.1 copy.17
  62.8 4.0 %gather_fusion = bf16[1024,512]{1,0:T(8,128)(2,1)S(1)} fusion(bf16[512,128]{0,1:T(8,128)(2,1)S(1)} %copy.17, s32[1024]{0:T(1024)S(1)} %broadcast_clamp_fusion.2), kind=kCustom, calls=%fused_computation.clone.clone.1 | custom fusion | bytes 2101248 | tf_op jit(solution)/shard_map/while/body/gather | solution.py:77
  66.7 0.1 dynamic_slice.22
  66.8 0.1 dynamic_slice.23
  66.9 6.2 %convolution_add_fusion.2 = f32[1024,1152]{1,0:T(8,128)} fusion(f32[1024,1152]{1,0:T(8,128)} %get-tuple-element.152, s32[512]{0:T(512)S(1)} %dynamic_slice.22, bf16[1024,512]{1,0:T(8,128)(2,1)S(1)} %gather_fusion, s32[512]{0:T(512)S(1)} %dynamic_slice.23, s32[1024]{0:T(1024)S(1)} %add_select_fusion.2), kind=kOutput, calls=%fused_computation.6.clone.1 | convolution fusion | flops 1210777600 | bytes 10493952 | tf_op jit(solution)/shard_map/while/body/tc,tb->cb/dot_general | solution.py:81
  73.1 4.0 %convert_element_type.22 = bf16[1024,1152]{1,0:T(8,128)(2,1)} convert(f32[1024,1152]{1,0:T(8,128)} %get-tuple-element.51) | non-fusion elementwise | flops 1179648 | bytes 7077888 | tf_op jit(solution)/shard_map/convert_element_type | solution.py:94
  77.1 70.1 %all-to-all-start = ((bf16[16,64,1152]{2,1,0:T(8,128)(2,1)}), bf16[16,64,1152]{2,1,0:T(8,128)(2,1)S(1)}, u32[]{:S(2)}, u32[]{:S(2)}) async-start(bf16[16,64,1152]{2,1,0:T(8,128)(2,1)} %bitcast.1), calls=%async_computation | async-start | bytes 4718592 | tf_op jit(solution)/shard_map/all_to_all | solution.py:17
  147.2 35.8 %all-to-all-done = bf16[16,64,1152]{2,1,0:T(8,128)(2,1)S(1)} async-done(((bf16[16,64,1152]{2,1,0:T(8,128)(2,1)}), bf16[16,64,1152]{2,1,0:T(8,128)(2,1)S(1)}, u32[]{:S(2)}, u32[]{:S(2)}) %all-to-all-start) | async-done | bytes 2359328 | tf_op jit(solution)/shard_map/all_to_all | solution.py:17
  183.0 0.3 convert_reduce_fusion
  183.3 5.6 %multiply_reduce_fusion = (f32[64]{0:T(128)S(1)}, f32[64,1152]{1,0:T(8,128)S(1)}) fusion(f32[64,1152]{1,0:T(8,128)S(1)} %convert_reduce_fusion, f32[1152,1152]{1,0:T(8,128)} %param.17), kind=kOutput, calls=%fused_computation.38 | convolution fusion | flops 1019363264 | bytes 5898496 | tf_op jit(solution)/shard_map/dot_general | solution.py:98
  188.9 0.8 rsqrt_multiply_fusion
  189.7 0.6 broadcast_in_dim.49
  190.3 3.5 %all-to-all-start.1 = ((f32[16,1,64]{2,1,0:T(1,128)}), f32[16,1,64]{2,1,0:T(1,128)S(1)}, u32[]{:S(2)}, u32[]{:S(2)}) async-start(f32[16,1,64]{2,1,0:T(1,128)} %broadcast_in_dim.49), calls=%async_computation.1 | async-start | bytes 16384 | tf_op jit(solution)/shard_map/all_to_all | solution.py:29
  193.8 0.1 multiply_convert_fusion
  193.9 7.4 %all-to-all-done.1 = f32[16,1,64]{2,1,0:T(1,128)S(1)} async-done(((f32[16,1,64]{2,1,0:T(1,128)}), f32[16,1,64]{2,1,0:T(1,128)S(1)}, u32[]{:S(2)}, u32[]{:S(2)}) %all-to-all-start.1) | async-done | bytes 4128 | tf_op jit(solution)/shard_map/all_to_all | solution.py:29
  201.3 1.7 broadcast_in_dim.73
  203.0 3.9 %all-to-all-start.2 = ((bf16[16,64,1152]{2,1,0:T(8,128)(2,1)}), bf16[16,64,1152]{2,1,0:T(8,128)(2,1)S(1)}, u32[]{:S(2)}, u32[]{:S(2)}) async-start(bf16[16,64,1152]{2,1,0:T(8,128)(2,1)} %broadcast_in_dim.73), calls=%async_computation.2 | async-start | bytes 4718592 | tf_op jit(solution)/shard_map/all_to_all | solution.py:29
  206.9 0.1 mul.47
  207.0 0.1 multiply_reduce_fusion.1
  207.1 0.1 reduce_sum.46
  207.2 0.1 reduce_sum.47
  207.3 13.8 %psum.7 = f32[8]{0:T(128)S(1)} all-reduce(f32[8]{0:T(128)S(1)} %reduce_sum.47), channel_id=1, replica_groups=mesh['trade'=16,'path'=8] {'path'}, use_global_device_ids=true, to_apply=%region_6.7 | all-reduce | flops 8 | bytes 64 | tf_op jit(solution)/shard_map/psum | solution.py:119
  221.2 0.5 broadcast.109
  221.7 0.7 reduce.5
  222.4 0.7 reshape_reshape.3
  223.0 0.5 broadcast_multiply_fusion
  223.5 14.7 %all-to-all-done.2 = bf16[16,64,1152]{2,1,0:T(8,128)(2,1)S(1)} async-done(((bf16[16,64,1152]{2,1,0:T(8,128)(2,1)}), bf16[16,64,1152]{2,1,0:T(8,128)(2,1)S(1)}, u32[]{:S(2)}, u32[]{:S(2)}) %all-to-all-start.2) | async-done | bytes 2359328 | tf_op jit(solution)/shard_map/all_to_all | solution.py:29
  238.3 13.3 %select_reduce_fusion = f32[4096,128]{1,0:T(8,128)S(1)} fusion(pred[4096,8]{0,1:T(8,128)(4,1)S(1)} %iota_compare_fusion.3, bf16[8,128,1152]{2,1,0:T(8,128)(2,1)S(1)} %bitcast.29, s32[4096]{0:T(1024)S(1)} %get-tuple-element.175), kind=kOutput, calls=%fused_computation.32 | convolution fusion | flops 9676259328 | bytes 4505600 | tf_op jit(solution)/shard_map/tb,cb->tc/dot_general | solution.py:107
  251.6 2.4 select_convert_fusion
  (15 shorter events, 0.1 us)
Async XLA Ops:
  0.6 1.4 copy-start
  2.1 23.1 %copy-start.1 = (s32[13824]{0:T(1024)S(1)}, s32[13824]{0:T(1024)}, u32[]{:S(2)}) copy-start(s32[13824]{0:T(1024)} %param.14) | copy-start | bytes 165892
  25.1 23.1 %copy-start.2 = (bf16[4096,128]{1,0:T(8,128)(2,1)S(1)}, bf16[4096,128]{1,0:T(8,128)(2,1)}, u32[]{:S(2)}) copy-start(bf16[4096,128]{1,0:T(8,128)(2,1)} %param.11) | copy-start | bytes 3145732
  49.6 2.4 copy-start.3
  77.1 105.9 %all-to-all-start = ((bf16[16,64,1152]{2,1,0:T(8,128)(2,1)}), bf16[16,64,1152]{2,1,0:T(8,128)(2,1)S(1)}, u32[]{:S(2)}, u32[]{:S(2)}) async-start(bf16[16,64,1152]{2,1,0:T(8,128)(2,1)} %bitcast.1), calls=%async_computation | async-start | bytes 4718592 | tf_op jit(solution)/shard_map/all_to_all | solution.py:17
  190.3 11.0 %all-to-all-start.1 = ((f32[16,1,64]{2,1,0:T(1,128)}), f32[16,1,64]{2,1,0:T(1,128)S(1)}, u32[]{:S(2)}, u32[]{:S(2)}) async-start(f32[16,1,64]{2,1,0:T(1,128)} %broadcast_in_dim.49), calls=%async_computation.1 | async-start | bytes 16384 | tf_op jit(solution)/shard_map/all_to_all | solution.py:29
  203.0 3.9 %copy-start.4 = (f32[128]{0:T(128)S(1)}, f32[128]{0:T(128)}, u32[]{:S(2)}) copy-start(f32[128]{0:T(128)} %param.18) | copy-start | bytes 1540
  203.0 35.3 %all-to-all-start.2 = ((bf16[16,64,1152]{2,1,0:T(8,128)(2,1)}), bf16[16,64,1152]{2,1,0:T(8,128)(2,1)S(1)}, u32[]{:S(2)}, u32[]{:S(2)}) async-start(bf16[16,64,1152]{2,1,0:T(8,128)(2,1)} %broadcast_in_dim.73), calls=%async_computation.2 | async-start | bytes 4718592 | tf_op jit(solution)/shard_map/all_to_all | solution.py:29
where the time goes:
time: 254 us
  starting transfers between devices  77.5 us (31%)
  local copies, waits for them, and re-layouts  60.7 us (24%)
  waiting for transfers between devices  57.9 us (23%)
  matrix products  31.3 us (12%)
  blocking collectives  13.8 us (5%)
  other arithmetic  11.3 us (4%)
    all_to_all x1, starting transfers between devices, summed_on_arrival(): lax.all_to_all(tiles, axis, split_axis=0, concat_axis=0, tiled=True)  70.1 us
    all_to_all x1, waiting for transfers between devices, summed_on_arrival(): lax.all_to_all(tiles, axis, split_axis=0, concat_axis=0, tiled=True)  35.8 us
    gather x1, local copies, waits for them, and re-layouts, shards(): trade_weight = risk_weight[block_ids]  23 us
    gather x1, local copies, waits for them, and re-layouts, shards(): trade_bucket = bucket_map[block_ids]  23 us
    all_to_all x2, waiting for transfers between devices, from_everyone(): lax.all_to_all(jnp.broadcast_to(x[None], (size, *x.shape)), axis, 0, 0, t...  22.2 us
    psum x1, blocking collectives, shards(): lax.psum(weighted_sum, 'path') / (path_count * lax.axis_size('path'))  13.8 us
    dot_general x1, matrix products, shards(): jnp.einsum('tb,cb->tc', all_hot, gather_directly(bucket_grad, 'trade', 0)...  13.3 us
    dot_general x2, matrix products, add_block(): jnp.einsum('tc,tb->cb', delta_rows, bucket_hot, preferred_element_type=jn...  12.5 us
  transfers between devices with their start and end apart: 3, of which 3 were waited for; matrix products, arithmetic and copies ran while one was open for 1% of the time, Pallas kernels for 0%

commit v1 on v0

v1 whole, which is shorter than its diff:
```python
import functools

import jax
import jax.numpy as jnp
from jax import lax
from jax.experimental import pallas as pl
from jax.experimental.pallas import tpu as pltpu
from jax.sharding import PartitionSpec as P

EPSILON = 1e-06
LANES = 128
F32 = jnp.float32
BF16 = jnp.bfloat16
MESH = pl.DeviceIdType.MESH
SIDE = 4
OTHERS = SIDE - 1
CHUNK = 512
NT = (((1,), (1,)), ((), ()))
NN = (((1,), (0,)), ((), ()))
TN = (((0,), (0,)), ((), ()))


def dot(a, b, dims):
    return lax.dot_general(a, b, dims, preferred_element_type=F32)


def tiles_of(total):
    cuts, at = [], 0
    while at < total:
        width = min(256, total - at)
        cuts.append((at, width))
        at += width
    return cuts


def kernel(
    groups,
    slabs,
    deltas,
    nets,
    blocks,
    rw,
    bm,
    counts,
    corr,
    pw,
    cot,
    margin_o,
    expected_o,
    grad_o,
    table,
    hot,
    X,
    wrow,
    S,
    recv1,
    st,
    recv2,
    SF,
    C,
    Chi,
    Clo,
    G,
    acc,
    m_send,
    m_recv,
    e_send,
    e_recv,
    c_sem,
    s_sems,
    r_sems,
    ms_sems,
    mr_sems,
    es_sems,
    er_sems,
):
    me = lax.axis_index("trade")
    slab = lax.axis_index("path")
    y, x = me // SIDE, me % SIDE
    capacity = deltas.shape[0]
    bucket_count = corr.shape[0]
    net_count, paths = cot.shape
    rows = net_count * paths
    own_rows = rows // groups
    tiles = tiles_of(bucket_count)

    barrier = pltpu.get_barrier_semaphore()
    for d in range(1, groups):
        pl.semaphore_signal(barrier, inc=1, device_id={"trade": (me + d) % groups}, device_id_type=MESH)
    for d in range(1, slabs):
        pl.semaphore_signal(barrier, inc=1, device_id={"path": (slab + d) % slabs}, device_id_type=MESH)

    c_copy = pltpu.make_async_copy(corr, C, c_sem)
    c_copy.start()

    table_rows = rw.shape[0]
    table[...] = jnp.zeros_like(table)
    w_all = rw[...]
    w1 = w_all.astype(BF16)
    w2 = (w_all - w1.astype(F32)).astype(BF16)
    b_all = bm[...]
    table[0:table_rows, 0:LANES] = w1
    table[0:table_rows, LANES : 2 * LANES] = w2
    table[0:table_rows, 2 * LANES : 3 * LANES] = (b_all // LANES).astype(F32).astype(BF16)
    table[0:table_rows, 3 * LANES : 4 * LANES] = (b_all % LANES).astype(F32).astype(BF16)
    live_count = counts[0]

    def look_up(i, carry):
        at = pl.multiple_of(i * CHUNK, CHUNK)
        ids = blocks[:, pl.ds(at, CHUNK)]
        high, low = ids // LANES, ids % LANES
        sub = lax.broadcasted_iota(jnp.int32, (LANES, CHUNK), 0)
        pick = jnp.where(sub == high, 1.0, 0.0).astype(BF16)
        found = dot(table[...], pick, TN)
        keep = sub == low
        parts = [
            jnp.sum(jnp.where(keep, found[k * LANES : (k + 1) * LANES], 0.0), axis=0, keepdims=True)
            for k in range(4)
        ]
        slot = at + lax.broadcasted_iota(jnp.int32, (1, CHUNK), 1)
        w = jnp.where(slot < live_count, parts[0] + parts[1], 0.0)
        wrow[0:1, pl.ds(at, CHUNK)] = w
        wrow[1:2, pl.ds(at, CHUNK)] = parts[2] * LANES + parts[3]
        turned = deltas[pl.ds(at, CHUNK), :].astype(F32).T
        weighted = (turned * w).astype(BF16)
        net = nets[:, pl.ds(at, CHUNK)]
        for n in range(net_count):
            mask = jnp.where(net == n, 1.0, 0.0).astype(BF16)
            X[n * paths : (n + 1) * paths, pl.ds(at, CHUNK)] = weighted * mask
        return carry

    lax.fori_loop(0, capacity // CHUNK, look_up, 0)

    def send(src, dst, phase, tile, d, peer):
        copy = pltpu.make_async_remote_copy(
            src_ref=src,
            dst_ref=dst,
            send_sem=s_sems.at[phase, tile, d - 1],
            recv_sem=r_sems.at[phase, tile, d - 1],
            device_id={"trade": peer},
            device_id_type=MESH,
        )
        copy.start()
        return copy

    def row_mate(d):
        return (x + d) % SIDE

    def column_mate(d):
        return (y + d) % SIDE

    def first_stage(t):
        at, width = tiles[t]
        cols = pl.ds(at, width)
        copies = []
        for d in (2, 1, 3):
            kx, ky = row_mate(d), column_mate(d)
            copies.append(send(S.at[:, kx, 0, :, cols], recv1.at[0, d - 1, :, :, cols], 0, t, d, y * SIDE + kx))
            copies.append(send(S.at[ky, :, 1, :, cols], recv1.at[1, d - 1, :, :, cols], 1, t, d, ky * SIDE + x))
        return copies

    def second_stage(t, arriving):
        at, width = tiles[t]
        cols = pl.ds(at, width)
        for copy in arriving:
            copy.wait_recv()
        total_a = S[:, x, 0, :, cols].astype(F32)
        total_b = S[y, :, 1, :, cols].astype(F32)
        for d in range(OTHERS):
            total_a += recv1[0, d, :, :, cols].astype(F32)
            total_b += recv1[1, d, :, :, cols].astype(F32)
        st[0, :, :, cols] = total_a.astype(BF16)
        st[1, :, :, cols] = total_b.astype(BF16)
        copies = []
        for d in (2, 1, 3):
            kx, ky = row_mate(d), column_mate(d)
            copies.append(send(st.at[0, ky, :, cols], recv2.at[0, d - 1, :, cols], 2, t, d, ky * SIDE + x))
            copies.append(send(st.at[1, kx, :, cols], recv2.at[1, d - 1, :, cols], 3, t, d, y * SIDE + kx))
        return copies

    def forward(t):
        at, width = tiles[t]
        for i in range(capacity // CHUNK):
            part = pl.ds(i * CHUNK, CHUNK)
            bucket = wrow[1:2, part]
            sub = (at + lax.broadcasted_iota(jnp.int32, (width, CHUNK), 0)).astype(F32)
            hot[at : at + width, part] = jnp.where(sub == bucket, 1.0, 0.0).astype(BF16)
        result = dot(X[...], hot[at : at + width, :], NT)
        S[:, :, :, :, at : at + width] = result.astype(BF16).reshape(S.shape[:-1] + (width,))

    sent = []
    stage1, stage2 = [], []
    for t in range(len(tiles)):
        forward(t)
        if t == 0:
            pl.semaphore_wait(barrier, groups - 1 + slabs - 1)
        stage1.append(first_stage(t))
        if t >= 1:
            stage2.append(second_stage(t - 1, stage1[t - 1]))
    c_copy.wait()
    for at, width in tiles:
        block = C[:, at : at + width]
        high = block.astype(BF16)
        Chi[:, at : at + width] = high
        Clo[:, at : at + width] = (block - high.astype(F32)).astype(BF16)
    stage2.append(second_stage(len(tiles) - 1, stage1[-1]))
    for t, (at, width) in enumerate(tiles):
        for copy in stage2[t]:
            copy.wait_recv()
        cols = pl.ds(at, width)
        total_a = st[0, y, :, cols].astype(F32)
        total_b = st[1, x, :, cols].astype(F32)
        for d in range(OTHERS):
            total_a += recv2[0, d, :, cols].astype(F32)
            total_b += recv2[1, d, :, cols].astype(F32)
        SF[0 : own_rows // 2, cols] = total_a
        SF[own_rows // 2 : own_rows, cols] = total_b

    summed = SF[...]
    s_high = summed.astype(BF16)
    s_low = (summed - s_high.astype(F32)).astype(BF16)
    both = dot(jnp.concatenate([s_high, s_low], axis=0), Chi[...], NN)
    coupled = both[0:own_rows] + both[own_rows:] + dot(s_high, Clo[...], NN)
    margin = jnp.sqrt(jnp.sum(summed * coupled, axis=1, keepdims=True) + EPSILON)
    per_net = paths // own_rows
    own_net, own_part = me // per_net, me % per_net
    sub = lax.broadcasted_iota(jnp.int32, (own_rows, paths), 0)
    lane = lax.broadcasted_iota(jnp.int32, (own_rows, paths), 1)
    mine = lane == sub + own_part * own_rows
    net_sub = lax.broadcasted_iota(jnp.int32, (net_count, paths), 0)
    cot_row = jnp.sum(jnp.where(net_sub == own_net, cot[...], 0.0), axis=0, keepdims=True)
    cot_column = jnp.sum(jnp.where(mine, cot_row, 0.0), axis=1, keepdims=True)
    grad = ((cot_column / margin) * coupled).astype(BF16)
    G[y, x] = grad.reshape(2, own_rows // 2, bucket_count)

    gather1, gather2 = [], []
    for t, (at, width) in enumerate(tiles):
        cols = pl.ds(at, width)
        copies = []
        for d in (2, 1, 3):
            kx, ky = row_mate(d), column_mate(d)
            own_a, own_b = G.at[y, x, 0, :, cols], G.at[y, x, 1, :, cols]
            copies.append(send(own_a, own_a, 4, t, d, ky * SIDE + x))
            copies.append(send(own_b, own_b, 5, t, d, y * SIDE + kx))
        gather1.append(copies)

    margin_row = jnp.sum(jnp.where(mine, margin, 0.0), axis=0, keepdims=True)
    my_margins = jnp.where(net_sub == own_net, margin_row, 0.0)
    m_send[...] = my_margins
    m_copies = []
    for d in range(1, groups):
        copy = pltpu.make_async_remote_copy(
            src_ref=m_send,
            dst_ref=m_recv.at[d - 1],
            send_sem=ms_sems.at[d - 1],
            recv_sem=mr_sems.at[d - 1],
            device_id={"trade": (me + d) % groups},
            device_id_type=MESH,
        )
        copy.start()
        m_copies.append(copy)

    def gather_second(t):
        at, width = tiles[t]
        cols = pl.ds(at, width)
        for copy in gather1[t]:
            copy.wait_recv()
        copies = []
        for d in (2, 1, 3):
            kx, ky = row_mate(d), column_mate(d)
            all_a, all_b = G.at[:, x, 0, :, cols], G.at[y, :, 1, :, cols]
            copies.append(send(all_a, all_a, 6, t, d, y * SIDE + kx))
            copies.append(send(all_b, all_b, 7, t, d, ky * SIDE + x))
        return copies

    def backward(t):
        at, width = tiles[t]
        step = 256

        def one(i, carry):
            start = pl.multiple_of(i * step, step)
            part = pl.ds(start, step)
            all_grad = G[:, :, :, :, at : at + width].reshape(rows, width)
            looked_up = dot(all_grad, hot[at : at + width, part], NN)
            net = nets[:, part]
            total = jnp.zeros((paths, step), F32) if t == 0 else acc[:, part]
            for n in range(net_count):
                total += jnp.where(net == n, looked_up[n * paths : (n + 1) * paths], 0.0)
            acc[:, part] = total
            return carry

        lax.fori_loop(0, capacity // step, one, 0)

    e_copies = []
    for t in range(len(tiles)):
        gather2.append(gather_second(t))
    for copy in m_copies:
        copy.wait_recv()
    all_margins = my_margins
    for d in range(groups - 1):
        all_margins += m_recv[d]
    margin_o[...] = all_margins
    my_sum = jnp.sum(all_margins * pw[...], axis=1, keepdims=True)
    e_send[...] = jnp.broadcast_to(my_sum, e_send.shape)
    for d in range(1, slabs):
        copy = pltpu.make_async_remote_copy(
            src_ref=e_send,
            dst_ref=e_recv.at[d - 1],
            send_sem=es_sems.at[d - 1],
            recv_sem=er_sems.at[d - 1],
            device_id={"path": (slab + d) % slabs},
            device_id_type=MESH,
        )
        copy.start()
        e_copies.append(copy)

    for t in range(len(tiles)):
        for copy in gather2[t]:
            copy.wait_recv()
        backward(t)

    def finish(i, carry):
        at = pl.multiple_of(i * CHUNK, CHUNK)
        part = pl.ds(at, CHUNK)
        scaled = acc[:, part] * wrow[0:1, part]
        grad_o[part, :] = scaled.T.astype(BF16)
        return carry

    lax.fori_loop(0, capacity // CHUNK, finish, 0)

    for copy in e_copies:
        copy.wait_recv()
    everyone = e_send[...]
    for d in range(slabs - 1):
        everyone += e_recv[d]
    expected_o[...] = everyone / (paths * slabs)

    for group in stage1 + stage2 + gather1 + gather2:
        for copy in group:
            copy.wait_send()
    for copy in m_copies + e_copies:
        copy.wait_send()


def shards(groups, slabs, deltas, net_ids, block_ids, bucket_map, risk_weight, counts, correlation, path_weight, margin_cotangent):
    capacity, paths = deltas.shape
    buckets = correlation.shape[0]
    net_count = margin_cotangent.shape[0]
    rows = net_count * paths
    half = rows // groups // 2
    tile_count = len(tiles_of(buckets))
    vmem = pl.BlockSpec(memory_space=pltpu.VMEM)
    smem = pl.BlockSpec(memory_space=pltpu.SMEM)
    dma = pltpu.SemaphoreType.DMA
    margin, expected, trade_grad = pl.pallas_call(
        functools.partial(kernel, groups, slabs),
        out_shape=(
            jax.ShapeDtypeStruct((net_count, paths), F32),
            jax.ShapeDtypeStruct((net_count, paths), F32),
            jax.ShapeDtypeStruct((capacity, paths), BF16),
        ),
        in_specs=[vmem, vmem, vmem, vmem, vmem, smem, pl.BlockSpec(memory_space=pl.ANY), vmem, vmem],
        out_specs=(vmem, vmem, vmem),
        scratch_shapes=[
            pltpu.VMEM((LANES, 4 * LANES), BF16),
            pltpu.VMEM((buckets, capacity), BF16),
            pltpu.VMEM((rows, capacity), BF16),
            pltpu.VMEM((2, capacity), F32),
            pltpu.VMEM((SIDE, SIDE, 2, half, buckets), BF16),
            pltpu.VMEM((2, OTHERS, SIDE, half, buckets), BF16),
            pltpu.VMEM((2, SIDE, half, buckets), BF16),
            pltpu.VMEM((2, OTHERS, half, buckets), BF16),
            pltpu.VMEM((2 * half, buckets), F32),
            pltpu.VMEM((buckets, buckets), F32),
            pltpu.VMEM((buckets, buckets), BF16),
            pltpu.VMEM((buckets, buckets), BF16),
            pltpu.VMEM((SIDE, SIDE, 2, half, buckets), BF16),
            pltpu.VMEM((paths, capacity), F32),
            pltpu.VMEM((net_count, paths), F32),
            pltpu.VMEM((groups - 1, net_count, paths), F32),
            pltpu.VMEM((net_count, paths), F32),
            pltpu.VMEM((slabs - 1, net_count, paths), F32),
            dma,
            dma((8, tile_count, OTHERS)),
            dma((8, tile_count, OTHERS)),
            dma((groups - 1,)),
            dma((groups - 1,)),
            dma((slabs - 1,)),
            dma((slabs - 1,)),
        ],
        compiler_params=pltpu.CompilerParams(
            collective_id=0, has_side_effects=True, vmem_limit_bytes=60 * 1024 * 1024
        ),
        name="margin_exchange",
    )(
        deltas,
        net_ids.reshape(1, capacity),
        block_ids.reshape(1, capacity),
        risk_weight.reshape(-1, LANES),
        bucket_map.reshape(-1, LANES),
        counts,
        correlation,
        path_weight.reshape(1, paths),
        margin_cotangent,
    )
    return margin, expected[:, 0], trade_grad


def solution(mesh):
    placed = (
        P("trade", "path"),
        P("trade"),
        P("trade"),
        P(),
        P(),
        P("trade"),
        P(),
        P("path"),
        P(None, "path"),
    )
    return jax.shard_map(
        functools.partial(shards, mesh.shape["trade"], mesh.shape["path"]),
        mesh=mesh,
        in_specs=placed,
        out_specs=(P(None, "path"), P(), P("trade", "path")),
        check_vma=False,
    )
```

time: 254 us -> 87.1 us (0.34)
  Pallas kernels: 0 us -> 80.7 us
  starting transfers between devices: 77.5 us -> 0 us
  waiting for transfers between devices: 57.9 us -> 0 us
  local copies, waits for them, and re-layouts: 60.7 us -> 4.83 us
  matrix products: 31.3 us -> 0 us
  blocking collectives: 13.8 us -> 0 us
  other arithmetic: 11.3 us -> 0 us
    pallas_call x0 -> x1, Pallas kernels: none -> 80.7 us  [shards(): pl.pallas_call(functools.partial(kernel, groups, slabs), out_shape=(jax.S...]
    all_to_all x3 -> x0, starting transfers between devices: 77.5 us -> none  [the longest x1 70.1 us: summed_on_arrival(): lax.all_to_all(tiles, axis, split_axis=0, concat_axis=0, tiled=True)]
    all_to_all x3 -> x0, waiting for transfers between devices: 57.9 us -> none  [the longest x1 35.8 us: summed_on_arrival(): lax.all_to_all(tiles, axis, split_axis=0, concat_axis=0, tiled=True)]
    gather x4 -> x0, local copies, waits for them, and re-layouts: 54 us -> none  [the longest x1 23 us: shards(): trade_weight = risk_weight[block_ids]]
    dot_general x4 -> x0, matrix products: 31.3 us -> none  [the longest x1 13.3 us: shards(): jnp.einsum('tb,cb->tc', all_hot, gather_directly(bucket_grad, 'trade', 0)...]
    psum x1 -> x0, blocking collectives: 13.8 us -> none  [shards(): lax.psum(weighted_sum, 'path') / (path_count * lax.axis_size('path'))]
    convert_element_type x4 -> x0, other arithmetic: 7.96 us -> none  [the longest x1 4.02 us: shards(): summed = summed_on_arrival(lax.fori_loop(0, live_blocks, advance, jnp.zer...]
    broadcast_in_dim x3 -> x0, local copies, waits for them, and re-layouts: 4.76 us -> none  [the longest x1 2.43 us: shards(): jnp.zeros((shard_len * lax.axis_size('trade'), bucket_count), jnp.float32)]
  transfers between devices with their start and end apart: 3 -> 0, of which waited for: 3 -> 0; matrix products, arithmetic and copies ran while one was open for 1% -> 0% of each run, Pallas kernels for 0% -> 0%
where the time goes in v1:
time: 87.1 us; the launch traced here: 86.9 us
  Pallas kernels  80.7 us (93%)
  local copies, waits for them, and re-layouts  4.83 us (6%)
  between operations  1.29 us (1%)
    pallas_call x1, Pallas kernels, shards(): pl.pallas_call(functools.partial(kernel, groups, slabs), out_shape=(jax.S...  80.7 us
    unnamed x2, local copies, waits for them, and re-layouts  3.53 us

profile of v1, /device:TPU:0, one launch (start us, length us, event | category | flops | bytes accessed | tf_op | source)
XLA Modules:
  0.0 86.9 jit_solution(14567283520335257604)
XLA Ops:
  1.3 80.7 %margin_exchange.1 = (f32[8,128]{1,0:T(8,128)}, f32[8,128]{1,0:T(8,128)}, bf16[4096,128]{1,0:T(8,128)(2,1)}) custom-call(bf16[4096,128]{1,0:T(8,128)(2,1)} %deltas.1, s32[1,4096]{1,0:T(1,128)} %bitcast.7, s32[1,4096]{1,0:T(1,128)} %bitcast.8, f32[108,128]{1,0:T(8,128)} %bitcast.5, s32[108,128]{1,0:T(8,128)} %bitcast.6, s32[1]{0:T(128)S(6)} %copy.14.counts, ...), custom_call_target="tpu_custom_call" | custom-call | tf_op jit(solution)/shard_map/margin_exchange/pallas_call | solution.py:355
  82.0 1.3 %slice_reduce_fusion = f32[8]{0:T(128)} fusion(f32[8,128]{1,0:T(8,128)} %get-tuple-element.7), kind=kLoop, calls=%fused_computation | loop fusion | bytes 64 | tf_op jit(solution)/shard_map/slice | solution.py:406
  83.3 1.3 %copy.15 = f32[8,128]{1,0:T(8,128)} copy(f32[8,128]{1,0:T(8,128)} %get-tuple-element.12) | data formatting | bytes 8192
  84.6 2.3 %copy.16 = bf16[4096,128]{1,0:T(8,128)(2,1)} copy(bf16[4096,128]{1,0:T(8,128)(2,1)} %get-tuple-element.14) | data formatting | bytes 2097152

commit v2 on v1

v2 whole, which is shorter than its diff:
```python
import functools

import jax
import jax.numpy as jnp
from jax import lax
from jax.experimental import pallas as pl
from jax.experimental.pallas import tpu as pltpu
from jax.sharding import PartitionSpec as P

EPSILON = 1e-06
LANES = 128
F32 = jnp.float32
BF16 = jnp.bfloat16
MESH = pl.DeviceIdType.MESH
SIDE = 4
OTHERS = SIDE - 1
CHUNK = 512
NT = (((1,), (1,)), ((), ()))
NN = (((1,), (0,)), ((), ()))
TN = (((0,), (0,)), ((), ()))


def dot(a, b, dims):
    return lax.dot_general(a, b, dims, preferred_element_type=F32)


TILE = 256


def tiles_of(total):
    cuts, at = [], 0
    while at < total:
        width = min(TILE, total - at)
        cuts.append((at, width))
        at += width
    return cuts


def kernel(
    groups,
    slabs,
    deltas,
    nets,
    blocks,
    rw,
    bm,
    counts,
    corr,
    pw,
    cot,
    margin_o,
    expected_o,
    weight_o,
    chosen_o,
    slots,
    table,
    hot,
    X,
    wrow,
    S,
    recv1,
    st,
    recv2,
    SF,
    C,
    Chi,
    Clo,
    G,
    acc,
    m_send,
    m_recv,
    e_send,
    e_recv,
    c_sem,
    d_sem,
    s_sems,
    r_sems,
    ms_sems,
    mr_sems,
    es_sems,
    er_sems,
):
    me = lax.axis_index("trade")
    slab = lax.axis_index("path")
    y, x = me // SIDE, me % SIDE
    capacity = deltas.shape[0]
    bucket_count = corr.shape[0]
    net_count, paths = cot.shape
    rows = net_count * paths
    own_rows = rows // groups
    tiles = tiles_of(bucket_count)

    barrier = pltpu.get_barrier_semaphore()
    for d in range(1, groups):
        pl.semaphore_signal(barrier, inc=1, device_id={"trade": (me + d) % groups}, device_id_type=MESH)
    for d in range(1, slabs):
        pl.semaphore_signal(barrier, inc=1, device_id={"path": (slab + d) % slabs}, device_id_type=MESH)

    d_copy = pltpu.make_async_copy(deltas, slots, d_sem)
    d_copy.start()
    c_copy = pltpu.make_async_copy(corr, C, c_sem)
    c_copy.start()

    table_rows = rw.shape[0]
    w_all = rw[...]
    w1 = w_all.astype(BF16).astype(F32)
    b_all = bm[...]
    parts = (w1, w_all - w1, (b_all // LANES).astype(F32), (b_all % LANES).astype(F32))
    table[...] = jnp.zeros_like(table)
    for k, part in enumerate(parts):
        table[k * LANES : (k + 1) * LANES, 0:table_rows] = part.T.astype(BF16)
    live_count = counts[0]
    acc[...] = jnp.zeros_like(acc)
    padded = hot.shape[0]
    if padded > bucket_count:
        G[:, :, :, :, bucket_count:padded] = jnp.zeros(G.shape[:-1] + (padded - bucket_count,), BF16)
    d_copy.wait()

    def look_up(i, carry):
        at = pl.multiple_of(i * CHUNK, CHUNK)
        ids = blocks[:, pl.ds(at, CHUNK)]
        high, low = ids // LANES, ids % LANES
        sub = lax.broadcasted_iota(jnp.int32, (LANES, CHUNK), 0)
        pick = jnp.where(sub == high, 1.0, 0.0).astype(BF16)
        found = dot(table[...], pick, NN)
        keep = sub == low
        parts = [
            jnp.sum(jnp.where(keep, found[k * LANES : (k + 1) * LANES], 0.0), axis=0, keepdims=True)
            for k in range(4)
        ]
        slot = at + lax.broadcasted_iota(jnp.int32, (1, CHUNK), 1)
        w = jnp.where(slot < live_count, parts[0] + parts[1], 0.0)
        weight_o[:, pl.ds(at, CHUNK)] = w
        wrow[:, pl.ds(at, CHUNK)] = parts[2] * LANES + parts[3]
        turned = slots[pl.ds(at, CHUNK), :].astype(F32).T
        weighted = (turned * w).astype(BF16)
        net = nets[:, pl.ds(at, CHUNK)]
        for n in range(net_count):
            mask = jnp.where(net == n, 1.0, 0.0).astype(BF16)
            X[n * paths : (n + 1) * paths, pl.ds(at, CHUNK)] = weighted * mask
        return carry

    lax.fori_loop(0, capacity // CHUNK, look_up, 0, unroll=2)

    def remote(src, dst, phase, tile, d, peer):
        return pltpu.make_async_remote_copy(
            src_ref=src,
            dst_ref=dst,
            send_sem=s_sems.at[phase, tile, d - 1],
            recv_sem=r_sems.at[phase, tile, d - 1],
            device_id={"trade": peer},
            device_id_type=MESH,
        )

    def mates(d):
        kx, ky = (x + d) % SIDE, (y + d) % SIDE
        return kx, ky, y * SIDE + kx, ky * SIDE + x

    def columns(t, width):
        at = t * TILE
        return pl.ds(at if isinstance(at, int) else pl.multiple_of(at, TILE), width)

    def stage1(t, width):
        cols = columns(t, width)
        for d in (2, 1, 3):
            kx, ky, in_row, in_column = mates(d)
            yield remote(S.at[:, kx, 0, :, cols], recv1.at[0, d - 1, :, :, cols], 0, t, d, in_row)
            yield remote(S.at[ky, :, 1, :, cols], recv1.at[1, d - 1, :, :, cols], 1, t, d, in_column)

    def stage2(t, width):
        cols = columns(t, width)
        for d in (2, 1, 3):
            kx, ky, in_row, in_column = mates(d)
            yield remote(st.at[0, ky, :, cols], recv2.at[0, d - 1, :, cols], 2, t, d, in_column)
            yield remote(st.at[1, kx, :, cols], recv2.at[1, d - 1, :, cols], 3, t, d, in_row)

    def gather1(t, width):
        cols = columns(t, width)
        own_a, own_b = G.at[y, x, 0, :, cols], G.at[y, x, 1, :, cols]
        for d in (2, 1, 3):
            kx, ky, in_row, in_column = mates(d)
            yield remote(own_a, own_a, 4, t, d, in_column)
            yield remote(own_b, own_b, 5, t, d, in_row)

    def gather2(t, width):
        cols = columns(t, width)
        all_a, all_b = G.at[:, x, 0, :, cols], G.at[y, :, 1, :, cols]
        for d in (2, 1, 3):
            kx, ky, in_row, in_column = mates(d)
            yield remote(all_a, all_a, 6, t, d, in_row)
            yield remote(all_b, all_b, 7, t, d, in_column)

    def start(copies):
        for copy in copies:
            copy.start()

    def arrive(copies):
        for copy in copies:
            copy.wait_recv()

    def pass_on(t, width):
        arrive(stage1(t, width))
        cols = columns(t, width)
        total_a = S[:, x, 0, :, cols].astype(F32)
        total_b = S[y, :, 1, :, cols].astype(F32)
        for d in range(OTHERS):
            total_a += recv1[0, d, :, :, cols].astype(F32)
            total_b += recv1[1, d, :, :, cols].astype(F32)
        st[0, :, :, cols] = total_a.astype(BF16)
        st[1, :, :, cols] = total_b.astype(BF16)
        start(stage2(t, width))

    last = len(tiles) - 1
    last_width = tiles[last][1]

    def forward(t, carry):
        at = pl.multiple_of(t * TILE, TILE)
        for i in range(capacity // CHUNK):
            part = pl.ds(i * CHUNK, CHUNK)
            bucket = wrow[:, part]
            sub = (at + lax.broadcasted_iota(jnp.int32, (TILE, CHUNK), 0)).astype(F32)
            hot[pl.ds(at, TILE), part] = jnp.where(sub == bucket, 1.0, 0.0).astype(BF16)
        result = dot(X[...], hot[pl.ds(at, TILE), :], NT)
        S[:, :, :, :, pl.ds(at, TILE)] = result.astype(BF16).reshape(S.shape[:-1] + (TILE,))

        @pl.when(t == 0)
        def _():
            pl.semaphore_wait(barrier, groups - 1 + slabs - 1)

        @pl.when(t < last)
        def _():
            start(stage1(t, TILE))

        @pl.when(t == last)
        def _():
            start(stage1(last, last_width))

        @pl.when(t > 0)
        def _():
            pass_on(t - 1, TILE)

        return carry

    lax.fori_loop(0, len(tiles), forward, 0)
    c_copy.wait()
    for at, width in tiles:
        block = C[:, at : at + width]
        high = block.astype(BF16)
        Chi[:, at : at + width] = high
        Clo[:, at : at + width] = (block - high.astype(F32)).astype(BF16)
    pass_on(last, last_width)
    for t, (at, width) in enumerate(tiles):
        arrive(stage2(t, width))
        cols = pl.ds(at, width)
        total_a = st[0, y, :, cols].astype(F32)
        total_b = st[1, x, :, cols].astype(F32)
        for d in range(OTHERS):
            total_a += recv2[0, d, :, cols].astype(F32)
            total_b += recv2[1, d, :, cols].astype(F32)
        SF[0 : own_rows // 2, cols] = total_a
        SF[own_rows // 2 : own_rows, cols] = total_b

    summed = SF[...]
    s_high = summed.astype(BF16)
    s_low = (summed - s_high.astype(F32)).astype(BF16)
    both = dot(jnp.concatenate([s_high, s_low], axis=0), Chi[...], NN)
    coupled = both[0:own_rows] + both[own_rows:] + dot(s_high, Clo[...], NN)
    margin = jnp.sqrt(jnp.sum(summed * coupled, axis=1, keepdims=True) + EPSILON)
    per_net = paths // own_rows
    own_net, own_part = me // per_net, me % per_net
    sub = lax.broadcasted_iota(jnp.int32, (own_rows, paths), 0)
    lane = lax.broadcasted_iota(jnp.int32, (own_rows, paths), 1)
    mine = lane == sub + own_part * own_rows
    net_sub = lax.broadcasted_iota(jnp.int32, (net_count, paths), 0)
    cot_row = jnp.sum(jnp.where(net_sub == own_net, cot[...], 0.0), axis=0, keepdims=True)
    cot_column = jnp.sum(jnp.where(mine, cot_row, 0.0), axis=1, keepdims=True)
    grad = ((cot_column / margin) * coupled).astype(BF16)
    G[y, x, :, :, 0:bucket_count] = grad.reshape(2, own_rows // 2, bucket_count)

    for t, (at, width) in enumerate(tiles):
        start(gather1(t, width))

    margin_row = jnp.sum(jnp.where(mine, margin, 0.0), axis=0, keepdims=True)
    my_margins = jnp.where(net_sub == own_net, margin_row, 0.0)
    m_send[...] = my_margins
    m_copies = []
    for d in range(1, groups):
        copy = pltpu.make_async_remote_copy(
            src_ref=m_send,
            dst_ref=m_recv.at[d - 1],
            send_sem=ms_sems.at[d - 1],
            recv_sem=mr_sems.at[d - 1],
            device_id={"trade": (me + d) % groups},
            device_id_type=MESH,
        )
        copy.start()
        m_copies.append(copy)

    for t, (at, width) in enumerate(tiles):
        arrive(gather1(t, width))
        start(gather2(t, width))
    e_copies = []
    for copy in m_copies:
        copy.wait_recv()
    all_margins = my_margins
    for d in range(groups - 1):
        all_margins += m_recv[d]
    margin_o[...] = all_margins
    my_sum = jnp.sum(all_margins * pw[...], axis=1, keepdims=True)
    e_send[...] = jnp.broadcast_to(my_sum, e_send.shape)
    for d in range(1, slabs):
        copy = pltpu.make_async_remote_copy(
            src_ref=e_send,
            dst_ref=e_recv.at[d - 1],
            send_sem=es_sems.at[d - 1],
            recv_sem=er_sems.at[d - 1],
            device_id={"path": (slab + d) % slabs},
            device_id_type=MESH,
        )
        copy.start()
        e_copies.append(copy)

    def backward(t, carry):
        @pl.when(t < last)
        def _():
            arrive(gather2(t, TILE))

        @pl.when(t == last)
        def _():
            arrive(gather2(last, last_width))

        at = pl.multiple_of(t * TILE, TILE)

        def one(i, carry):
            part = pl.ds(pl.multiple_of(i * CHUNK, CHUNK), CHUNK)
            all_grad = G[:, :, :, :, pl.ds(at, TILE)].reshape(rows, TILE)
            looked_up = dot(all_grad, hot[pl.ds(at, TILE), part], NN)
            net = nets[:, part]
            total = acc[:, part]
            for n in range(net_count):
                total += jnp.where(net == n, looked_up[n * paths : (n + 1) * paths], 0.0)
            acc[:, part] = total
            return carry

        return lax.fori_loop(0, capacity // CHUNK, one, carry, unroll=2)

    lax.fori_loop(0, len(tiles), backward, 0)
    chosen_o[...] = acc[...].astype(BF16)

    for copy in e_copies:
        copy.wait_recv()
    everyone = e_send[...]
    for d in range(slabs - 1):
        everyone += e_recv[d]
    expected_o[...] = everyone / (paths * slabs)

    for t, (at, width) in enumerate(tiles):
        for stage in (stage1, stage2, gather1, gather2):
            for copy in stage(t, width):
                copy.wait_send()
    for copy in m_copies + e_copies:
        copy.wait_send()


def finish(weight, chosen, margin, expected, grad_o, margin_o, expected_o):
    scaled = chosen[...].astype(F32) * weight[...]
    grad_o[...] = scaled.T.astype(BF16)
    margin_o[...] = margin[...]
    net_count = margin.shape[0]
    sub = lax.broadcasted_iota(jnp.int32, margin.shape, 0)
    lane = lax.broadcasted_iota(jnp.int32, margin.shape, 1)
    row = jnp.sum(jnp.where(sub == lane, expected[...], 0.0), axis=0, keepdims=True)
    expected_o[...] = row[:, 0:net_count]


def shards(groups, slabs, deltas, net_ids, block_ids, bucket_map, risk_weight, counts, correlation, path_weight, margin_cotangent):
    capacity, paths = deltas.shape
    buckets = correlation.shape[0]
    net_count = margin_cotangent.shape[0]
    rows = net_count * paths
    half = rows // groups // 2
    tile_count = len(tiles_of(buckets))
    padded = tile_count * TILE
    vmem = pl.BlockSpec(memory_space=pltpu.VMEM)
    smem = pl.BlockSpec(memory_space=pltpu.SMEM)
    dma = pltpu.SemaphoreType.DMA
    anywhere = pl.BlockSpec(memory_space=pl.ANY)
    margin, expected, weight, chosen = pl.pallas_call(
        functools.partial(kernel, groups, slabs),
        out_shape=(
            jax.ShapeDtypeStruct((net_count, paths), F32),
            jax.ShapeDtypeStruct((net_count, paths), F32),
            jax.ShapeDtypeStruct((1, capacity), F32),
            jax.ShapeDtypeStruct((paths, capacity), BF16),
        ),
        in_specs=[anywhere, vmem, vmem, vmem, vmem, smem, anywhere, vmem, vmem],
        out_specs=(vmem, vmem, vmem, vmem),
        scratch_shapes=[
            pltpu.VMEM((capacity, paths), BF16),
            pltpu.VMEM((4 * LANES, LANES), BF16),
            pltpu.VMEM((padded, capacity), BF16),
            pltpu.VMEM((rows, capacity), BF16),
            pltpu.VMEM((1, capacity), F32),
            pltpu.VMEM((SIDE, SIDE, 2, half, padded), BF16),
            pltpu.VMEM((2, OTHERS, SIDE, half, buckets), BF16),
            pltpu.VMEM((2, SIDE, half, buckets), BF16),
            pltpu.VMEM((2, OTHERS, half, buckets), BF16),
            pltpu.VMEM((2 * half, buckets), F32),
            pltpu.VMEM((buckets, buckets), F32),
            pltpu.VMEM((buckets, buckets), BF16),
            pltpu.VMEM((buckets, buckets), BF16),
            pltpu.VMEM((SIDE, SIDE, 2, half, padded), BF16),
            pltpu.VMEM((paths, capacity), F32),
            pltpu.VMEM((net_count, paths), F32),
            pltpu.VMEM((groups - 1, net_count, paths), F32),
            pltpu.VMEM((net_count, paths), F32),
            pltpu.VMEM((slabs - 1, net_count, paths), F32),
            dma,
            dma,
            dma((8, tile_count, OTHERS)),
            dma((8, tile_count, OTHERS)),
            dma((groups - 1,)),
            dma((groups - 1,)),
            dma((slabs - 1,)),
            dma((slabs - 1,)),
        ],
        compiler_params=pltpu.CompilerParams(
            collective_id=0, has_side_effects=True, vmem_limit_bytes=60 * 1024 * 1024
        ),
        name="margin_exchange",
    )(
        deltas,
        net_ids.reshape(1, capacity),
        block_ids.reshape(1, capacity),
        risk_weight.reshape(-1, LANES),
        bucket_map.reshape(-1, LANES),
        counts,
        correlation,
        path_weight.reshape(1, paths),
        margin_cotangent,
    )
    block = capacity // 4
    whole = pl.BlockSpec((net_count, paths), lambda i: (0, 0))
    trade_grad, margin, expected = pl.pallas_call(
        finish,
        grid=(capacity // block,),
        out_shape=(
            jax.ShapeDtypeStruct((capacity, paths), BF16),
            jax.ShapeDtypeStruct((net_count, paths), F32),
            jax.ShapeDtypeStruct((1, net_count), F32),
        ),
        in_specs=[
            pl.BlockSpec((1, block), lambda i: (0, i)),
            pl.BlockSpec((paths, block), lambda i: (0, i)),
            whole,
            whole,
        ],
        out_specs=(
            pl.BlockSpec((block, paths), lambda i: (i, 0)),
            whole,
            pl.BlockSpec((1, net_count), lambda i: (0, 0)),
        ),
        name="finish",
    )(weight, chosen, margin, expected)
    return margin, expected.reshape(net_count), trade_grad


def solution(mesh):
    placed = (
        P("trade", "path"),
        P("trade"),
        P("trade"),
        P(),
        P(),
        P("trade"),
        P(),
        P("path"),
        P(None, "path"),
    )
    return jax.shard_map(
        functools.partial(shards, mesh.shape["trade"], mesh.shape["path"]),
        mesh=mesh,
        in_specs=placed,
        out_specs=(P(None, "path"), P(), P("trade", "path")),
        check_vma=False,
    )
```

time: 87.1 us -> 70.5 us (0.81)
  Pallas kernels: 80.7 us -> 69 us
  local copies, waits for them, and re-layouts: 4.83 us -> 0 us
    pallas_call x1, Pallas kernels: 80.7 us -> 65.4 us  [shards(): pl.pallas_call(functools.partial(kernel, groups, slabs), out_shape=(jax.S...]
    pallas_call x0 -> x1, Pallas kernels: none -> 3.63 us  [shards(): pl.pallas_call(finish, grid=(capacity // block,), out_shape=(jax.ShapeDty...]
    unnamed x2 -> x0, local copies, waits for them, and re-layouts: 3.53 us -> none
    slice x1 -> x0, local copies, waits for them, and re-layouts: 1.3 us -> none  [shards(): return (margin, expected[:, 0], trade_grad)]
where the time goes in v2:
time: 70.5 us; the launch traced here: 70.3 us
  Pallas kernels  69 us (98%)
  between operations  1.29 us (2%)
    pallas_call x1, Pallas kernels, shards(): pl.pallas_call(functools.partial(kernel, groups, slabs), out_shape=(jax.S...  65.4 us
    pallas_call x1, Pallas kernels, shards(): pl.pallas_call(finish, grid=(capacity // block,), out_shape=(jax.ShapeDty...  3.63 us

profile of v2, /device:TPU:0, one launch (start us, length us, event | category | flops | bytes accessed | tf_op | source)
XLA Modules:
  0.0 70.3 jit_solution(15099649012694574178)
XLA Ops:
  1.3 65.4 %margin_exchange.1 = (f32[8,128]{1,0:T(8,128)}, f32[8,128]{1,0:T(8,128)}, f32[1,4096]{1,0:T(1,128)}, bf16[128,4096]{1,0:T(8,128)(2,1)}) custom-call(bf16[4096,128]{1,0:T(8,128)(2,1)} %deltas.1, s32[1,4096]{1,0:T(1,128)} %bitcast.8, s32[1,4096]{1,0:T(1,128)} %bitcast.9, f32[108,128]{1,0:T(8,128)} %bitcast.6, s32[108,128]{1,0:T(8,128)} %bitcast.7, ...), custom_call_target="tpu_custom_call" | custom-call | tf_op jit(solution)/shard_map/margin_exchange/pallas_call | solution.py:388
  66.6 3.6 %finish.1 = (bf16[4096,128]{1,0:T(8,128)(2,1)}, f32[8,128]{1,0:T(8,128)}, f32[1,8]{1,0:T(1,128)}) custom-call(f32[1,4096]{1,0:T(1,128)} %get-tuple-element.10.weight, bf16[128,4096]{1,0:T(8,128)(2,1)} %get-tuple-element.11.chosen, f32[8,128]{1,0:T(8,128)} %get-tuple-element.12.margin, f32[8,128]{1,0:T(8,128)} %get-tuple-element.13.expected), custom_call_target="tpu_custom_call" | custom-call | tf_op jit(solution)/shard_map/finish/pallas_call | solution.py:444

commit v3 on v2

--- a/solution.py
+++ b/solution.py
@@ -25,6 +25,8 @@
 
 
 TILE = 256
+LAG = 3
+STEP = 1024
 
 
 def tiles_of(total):
@@ -39,20 +41,26 @@
 def kernel(
     groups,
     slabs,
-    deltas,
+    deltas_in,
+    nets_in,
+    blocks_in,
+    rw_in,
+    bm_in,
+    counts,
+    corr,
+    pw_in,
+    cot_in,
+    margin_o,
+    expected_o,
+    grad_o,
+    slots,
     nets,
     blocks,
     rw,
     bm,
-    counts,
-    corr,
     pw,
     cot,
-    margin_o,
-    expected_o,
-    weight_o,
-    chosen_o,
-    slots,
+    weight,
     table,
     hot,
     X,
@@ -72,7 +80,7 @@
     e_send,
     e_recv,
     c_sem,
-    d_sem,
+    in_sems,
     s_sems,
     r_sems,
     ms_sems,
@@ -83,38 +91,53 @@
     me = lax.axis_index("trade")
     slab = lax.axis_index("path")
     y, x = me // SIDE, me % SIDE
-    capacity = deltas.shape[0]
+    capacity = slots.shape[0]
     bucket_count = corr.shape[0]
     net_count, paths = cot.shape
     rows = net_count * paths
     own_rows = rows // groups
     tiles = tiles_of(bucket_count)
 
+    entering = [
+        pltpu.make_async_copy(source, target, in_sems.at[i])
+        for i, (source, target) in enumerate(
+            (
+                (rw_in, rw),
+                (bm_in, bm),
+                (blocks_in, blocks),
+                (nets_in, nets),
+                (deltas_in, slots),
+                (pw_in, pw),
+                (cot_in, cot),
+            )
+        )
+    ]
+    for copy in entering:
+        copy.start()
+    c_copy = pltpu.make_async_copy(corr, C, c_sem)
+    c_copy.start()
+
     barrier = pltpu.get_barrier_semaphore()
     for d in range(1, groups):
         pl.semaphore_signal(barrier, inc=1, device_id={"trade": (me + d) % groups}, device_id_type=MESH)
     for d in range(1, slabs):
         pl.semaphore_signal(barrier, inc=1, device_id={"path": (slab + d) % slabs}, device_id_type=MESH)
 
-    d_copy = pltpu.make_async_copy(deltas, slots, d_sem)
-    d_copy.start()
-    c_copy = pltpu.make_async_copy(corr, C, c_sem)
-    c_copy.start()
-
+    acc[...] = jnp.zeros_like(acc)
+    table[...] = jnp.zeros_like(table)
+    padded = hot.shape[0]
+    if padded > bucket_count:
+        G[:, :, :, :, bucket_count:padded] = jnp.zeros(G.shape[:-1] + (padded - bucket_count,), BF16)
+    for copy in entering:
+        copy.wait()
     table_rows = rw.shape[0]
     w_all = rw[...]
     w1 = w_all.astype(BF16).astype(F32)
     b_all = bm[...]
     parts = (w1, w_all - w1, (b_all // LANES).astype(F32), (b_all % LANES).astype(F32))
-    table[...] = jnp.zeros_like(table)
     for k, part in enumerate(parts):
         table[k * LANES : (k + 1) * LANES, 0:table_rows] = part.T.astype(BF16)
     live_count = counts[0]
-    acc[...] = jnp.zeros_like(acc)
-    padded = hot.shape[0]
-    if padded > bucket_count:
-        G[:, :, :, :, bucket_count:padded] = jnp.zeros(G.shape[:-1] + (padded - bucket_count,), BF16)
-    d_copy.wait()
 
     def look_up(i, carry):
         at = pl.multiple_of(i * CHUNK, CHUNK)
@@ -130,9 +153,9 @@
         ]
         slot = at + lax.broadcasted_iota(jnp.int32, (1, CHUNK), 1)
         w = jnp.where(slot < live_count, parts[0] + parts[1], 0.0)
-        weight_o[:, pl.ds(at, CHUNK)] = w
+        weight[:, pl.ds(at, CHUNK)] = w
         wrow[:, pl.ds(at, CHUNK)] = parts[2] * LANES + parts[3]
-        turned = slots[pl.ds(at, CHUNK), :].astype(F32).T
+        turned = slots[pl.ds(at, CHUNK), :].T.astype(F32)
         weighted = (turned * w).astype(BF16)
         net = nets[:, pl.ds(at, CHUNK)]
         for n in range(net_count):
@@ -140,7 +163,7 @@
             X[n * paths : (n + 1) * paths, pl.ds(at, CHUNK)] = weighted * mask
         return carry
 
-    lax.fori_loop(0, capacity // CHUNK, look_up, 0, unroll=2)
+    lax.fori_loop(0, capacity // CHUNK, look_up, 0, unroll=4)
 
     def remote(src, dst, phase, tile, d, peer):
         return pltpu.make_async_remote_copy(
@@ -235,9 +258,9 @@
         def _():
             start(stage1(last, last_width))
 
-        @pl.when(t > 0)
-        def _():
-            pass_on(t - 1, TILE)
+        @pl.when(t >= LAG)
+        def _():
+            pass_on(t - LAG, TILE)
 
         return carry
 
@@ -248,7 +271,8 @@
         high = block.astype(BF16)
         Chi[:, at : at + width] = high
         Clo[:, at : at + width] = (block - high.astype(F32)).astype(BF16)
-    pass_on(last, last_width)
+    for t in range(len(tiles) - LAG, len(tiles)):
+        pass_on(t, tiles[t][1])
     for t, (at, width) in enumerate(tiles):
         arrive(stage2(t, width))
         cols = pl.ds(at, width)
@@ -277,50 +301,53 @@
     grad = ((cot_column / margin) * coupled).astype(BF16)
     G[y, x, :, :, 0:bucket_count] = grad.reshape(2, own_rows // 2, bucket_count)
 
-    for t, (at, width) in enumerate(tiles):
-        start(gather1(t, width))
+    for t in reversed(range(len(tiles))):
+        start(gather1(t, tiles[t][1]))
 
     margin_row = jnp.sum(jnp.where(mine, margin, 0.0), axis=0, keepdims=True)
     my_margins = jnp.where(net_sub == own_net, margin_row, 0.0)
     m_send[...] = my_margins
-    m_copies = []
-    for d in range(1, groups):
-        copy = pltpu.make_async_remote_copy(
-            src_ref=m_send,
-            dst_ref=m_recv.at[d - 1],
-            send_sem=ms_sems.at[d - 1],
-            recv_sem=mr_sems.at[d - 1],
-            device_id={"trade": (me + d) % groups},
-            device_id_type=MESH,
-        )
-        copy.start()
-        m_copies.append(copy)
-
-    for t, (at, width) in enumerate(tiles):
-        arrive(gather1(t, width))
-        start(gather2(t, width))
-    e_copies = []
-    for copy in m_copies:
-        copy.wait_recv()
-    all_margins = my_margins
-    for d in range(groups - 1):
-        all_margins += m_recv[d]
-    margin_o[...] = all_margins
-    my_sum = jnp.sum(all_margins * pw[...], axis=1, keepdims=True)
-    e_send[...] = jnp.broadcast_to(my_sum, e_send.shape)
-    for d in range(1, slabs):
-        copy = pltpu.make_async_remote_copy(
-            src_ref=e_send,
-            dst_ref=e_recv.at[d - 1],
-            send_sem=es_sems.at[d - 1],
-            recv_sem=er_sems.at[d - 1],
-            device_id={"path": (slab + d) % slabs},
-            device_id_type=MESH,
-        )
-        copy.start()
-        e_copies.append(copy)
-
-    def backward(t, carry):
+
+    def margin_copies():
+        for d in range(1, groups):
+            yield pltpu.make_async_remote_copy(
+                src_ref=m_send,
+                dst_ref=m_recv.at[d - 1],
+                send_sem=ms_sems.at[d - 1],
+                recv_sem=mr_sems.at[d - 1],
+                device_id={"trade": (me + d) % groups},
+                device_id_type=MESH,
+            )
+
+    for t in reversed(range(len(tiles))):
+        arrive(gather1(t, tiles[t][1]))
+        start(gather2(t, tiles[t][1]))
+        if t == last:
+            start(margin_copies())
+    def mean_copies():
+        for d in range(1, slabs):
+            yield pltpu.make_async_remote_copy(
+                src_ref=e_send,
+                dst_ref=e_recv.at[d - 1],
+                send_sem=es_sems.at[d - 1],
+                recv_sem=er_sems.at[d - 1],
+                device_id={"path": (slab + d) % slabs},
+                device_id_type=MESH,
+            )
+
+    def margins():
+        arrive(margin_copies())
+        all_margins = m_send[...]
+        for d in range(groups - 1):
+            all_margins += m_recv[d]
+        margin_o[...] = all_margins
+        my_sum = jnp.sum(all_margins * pw[...], axis=1, keepdims=True)
+        e_send[...] = jnp.broadcast_to(my_sum, e_send.shape)
+        start(mean_copies())
+
+    def backward(i, carry):
+        t = last - i
+
         @pl.when(t < last)
         def _():
             arrive(gather2(t, TILE))
@@ -332,7 +359,7 @@
         at = pl.multiple_of(t * TILE, TILE)
 
         def one(i, carry):
-            part = pl.ds(pl.multiple_of(i * CHUNK, CHUNK), CHUNK)
+            part = pl.ds(pl.multiple_of(i * STEP, STEP), STEP)
             all_grad = G[:, :, :, :, pl.ds(at, TILE)].reshape(rows, TILE)
             looked_up = dot(all_grad, hot[pl.ds(at, TILE), part], NN)
             net = nets[:, part]
@@ -342,13 +369,18 @@
             acc[:, part] = total
             return carry
 
-        return lax.fori_loop(0, capacity // CHUNK, one, carry, unroll=2)
+        lax.fori_loop(0, capacity // STEP, one, carry, unroll=2)
+
+        @pl.when(i == 1)
+        def _():
+            margins()
+
+        return carry
 
     lax.fori_loop(0, len(tiles), backward, 0)
-    chosen_o[...] = acc[...].astype(BF16)
-
-    for copy in e_copies:
-        copy.wait_recv()
+    grad_o[...] = (acc[...] * weight[...]).astype(BF16)
+
+    arrive(mean_copies())
     everyone = e_send[...]
     for d in range(slabs - 1):
         everyone += e_recv[d]
@@ -358,13 +390,14 @@
         for stage in (stage1, stage2, gather1, gather2):
             for copy in stage(t, width):
                 copy.wait_send()
-    for copy in m_copies + e_copies:
+    for copy in (*margin_copies(), *mean_copies()):
         copy.wait_send()
 
 
-def finish(weight, chosen, margin, expected, grad_o, margin_o, expected_o):
-    scaled = chosen[...].astype(F32) * weight[...]
-    grad_o[...] = scaled.T.astype(BF16)
+def finish(grad, margin, expected, grad_o, margin_o, expected_o):
+    block = grad_o.shape[0]
+    at = pl.multiple_of(pl.program_id(0) * block, block)
+    grad_o[...] = grad[:, pl.ds(at, block)].T
     margin_o[...] = margin[...]
     net_count = margin.shape[0]
     sub = lax.broadcasted_iota(jnp.int32, margin.shape, 0)
@@ -385,18 +418,24 @@
     smem = pl.BlockSpec(memory_space=pltpu.SMEM)
     dma = pltpu.SemaphoreType.DMA
     anywhere = pl.BlockSpec(memory_space=pl.ANY)
-    margin, expected, weight, chosen = pl.pallas_call(
+    margin, expected, turned_grad = pl.pallas_call(
         functools.partial(kernel, groups, slabs),
         out_shape=(
             jax.ShapeDtypeStruct((net_count, paths), F32),
             jax.ShapeDtypeStruct((net_count, paths), F32),
-            jax.ShapeDtypeStruct((1, capacity), F32),
             jax.ShapeDtypeStruct((paths, capacity), BF16),
         ),
-        in_specs=[anywhere, vmem, vmem, vmem, vmem, smem, anywhere, vmem, vmem],
-        out_specs=(vmem, vmem, vmem, vmem),
+        in_specs=[anywhere] * 5 + [smem] + [anywhere] * 3,
+        out_specs=(vmem, vmem, vmem),
         scratch_shapes=[
             pltpu.VMEM((capacity, paths), BF16),
+            pltpu.VMEM((1, capacity), jnp.int32),
+            pltpu.VMEM((1, capacity), jnp.int32),
+            pltpu.VMEM((risk_weight.size // LANES, LANES), F32),
+            pltpu.VMEM((bucket_map.size // LANES, LANES), jnp.int32),
+            pltpu.VMEM((1, paths), F32),
+            pltpu.VMEM((net_count, paths), F32),
+            pltpu.VMEM((1, capacity), F32),
             pltpu.VMEM((4 * LANES, LANES), BF16),
             pltpu.VMEM((padded, capacity), BF16),
             pltpu.VMEM((rows, capacity), BF16),
@@ -416,7 +455,7 @@
             pltpu.VMEM((net_count, paths), F32),
             pltpu.VMEM((slabs - 1, net_count, paths), F32),
             dma,
-            dma,
+            dma((7,)),
             dma((8, tile_count, OTHERS)),
             dma((8, tile_count, OTHERS)),
             dma((groups - 1,)),
@@ -425,7 +464,7 @@
             dma((slabs - 1,)),
         ],
         compiler_params=pltpu.CompilerParams(
-            collective_id=0, has_side_effects=True, vmem_limit_bytes=60 * 1024 * 1024
+            collective_id=0, has_side_effects=True, vmem_limit_bytes=52 * 1024 * 1024
         ),
         name="margin_exchange",
     )(
@@ -439,7 +478,7 @@
         path_weight.reshape(1, paths),
         margin_cotangent,
     )
-    block = capacity // 4
+    block = capacity // 2
     whole = pl.BlockSpec((net_count, paths), lambda i: (0, 0))
     trade_grad, margin, expected = pl.pallas_call(
         finish,
@@ -449,19 +488,15 @@
             jax.ShapeDtypeStruct((net_count, paths), F32),
             jax.ShapeDtypeStruct((1, net_count), F32),
         ),
-        in_specs=[
-            pl.BlockSpec((1, block), lambda i: (0, i)),
-            pl.BlockSpec((paths, block), lambda i: (0, i)),
-            whole,
-            whole,
-        ],
+        in_specs=[vmem, vmem, vmem],
         out_specs=(
             pl.BlockSpec((block, paths), lambda i: (i, 0)),
             whole,
             pl.BlockSpec((1, net_count), lambda i: (0, 0)),
         ),
+        compiler_params=pltpu.CompilerParams(vmem_limit_bytes=8 * 1024 * 1024),
         name="finish",
-    )(weight, chosen, margin, expected)
+    )(turned_grad, margin, expected)
     return margin, expected.reshape(net_count), trade_grad
 
 

time: 70.5 us -> 63.3 us (0.90)
  Pallas kernels: 69 us -> 57.2 us
  local copies, waits for them, and re-layouts: 0 us -> 4.41 us
    pallas_call x1, Pallas kernels: 65.4 us -> 56 us  [shards(): pl.pallas_call(functools.partial(kernel, groups, slabs), out_shape=(jax.S...]
    unnamed x0 -> x12, local copies, waits for them, and re-layouts: none -> 4.41 us
    pallas_call x1, Pallas kernels: 3.63 us -> 1.21 us  [shards(): pl.pallas_call(finish, grid=(capacity // block,), out_shape=(jax.ShapeDty...]
where the time goes in v3:
time: 63.3 us; the launch traced here: 62.9 us
  Pallas kernels  57.2 us (90%)
  local copies, waits for them, and re-layouts  4.41 us (7%)
  between operations  1.3 us (2%)
    pallas_call x1, Pallas kernels, shards(): pl.pallas_call(functools.partial(kernel, groups, slabs), out_shape=(jax.S...  56 us
    unnamed x12, local copies, waits for them, and re-layouts  4.41 us

profile of v3, /device:TPU:0, one launch (start us, length us, event | category | flops | bytes accessed | tf_op | source)
XLA Modules:
  0.0 62.9 jit_solution(6536435691749796050)
XLA Ops:
  1.3 0.0 copy-start
  1.3 0.8 %copy-done = f32[13824]{0:T(1024)S(1)} copy-done((f32[13824]{0:T(1024)S(1)}, f32[13824]{0:T(1024)}, u32[]{:S(2)}) %copy-start) | copy-done | bytes 55320
  2.1 0.0 copy-start.1
  2.1 0.8 %copy-done.1 = s32[13824]{0:T(1024)S(1)} copy-done((s32[13824]{0:T(1024)S(1)}, s32[13824]{0:T(1024)}, u32[]{:S(2)}) %copy-start.1) | copy-done | bytes 55320
  2.9 0.0 copy-start.2
  2.9 0.7 %copy-done.2 = s32[4096]{0:T(1024)S(1)} copy-done((s32[4096]{0:T(1024)S(1)}, s32[4096]{0:T(1024)}, u32[]{:S(2)}) %copy-start.2) | copy-done | bytes 16408
  3.6 0.0 copy-start.3
  3.6 0.7 %copy-done.3 = s32[4096]{0:T(1024)S(1)} copy-done((s32[4096]{0:T(1024)S(1)}, s32[4096]{0:T(1024)}, u32[]{:S(2)}) %copy-start.3) | copy-done | bytes 16408
  4.4 0.0 copy-start.4
  4.4 0.7 %copy-done.4 = f32[8,128]{1,0:T(8,128)S(1)} copy-done((f32[8,128]{1,0:T(8,128)S(1)}, f32[8,128]{1,0:T(8,128)}, u32[]{:S(2)}) %copy-start.4) | copy-done | bytes 4120
  5.0 0.0 copy-start.5
  5.0 0.7 %copy-done.5 = f32[128]{0:T(128)S(1)} copy-done((f32[128]{0:T(128)S(1)}, f32[128]{0:T(128)}, u32[]{:S(2)}) %copy-start.5) | copy-done | bytes 536
  5.7 56.0 %margin_exchange.1 = (f32[8,128]{1,0:T(8,128)S(1)}, f32[8,128]{1,0:T(8,128)S(1)}, bf16[128,4096]{1,0:T(8,128)(2,1)S(1)}) custom-call(bf16[4096,128]{1,0:T(8,128)(2,1)} %deltas_in.1, s32[1,4096]{1,0:T(1,128)S(1)} %bitcast.8, s32[1,4096]{1,0:T(1,128)S(1)} %bitcast.9, f32[108,128]{1,0:T(8,128)S(1)} %bitcast.6, s32[108,128]{1,0:T(8,128)S(1)} %bitcast.7, ...), custom_call_target="tpu_custom_call" | custom-call | tf_op jit(solution)/shard_map/margin_exchange/pallas_call | solution.py:421
  61.7 1.2 %finish.1 = (bf16[4096,128]{1,0:T(8,128)(2,1)}, f32[8,128]{1,0:T(8,128)}, f32[1,8]{1,0:T(1,128)}) custom-call(bf16[128,4096]{1,0:T(8,128)(2,1)S(1)} %get-tuple-element.9.grad, f32[8,128]{1,0:T(8,128)S(1)} %get-tuple-element.10.margin, f32[8,128]{1,0:T(8,128)S(1)} %get-tuple-element.11.expected), custom_call_target="tpu_custom_call" | custom-call | tf_op jit(solution)/shard_map/finish/pallas_call | solution.py:483
Async XLA Ops:
  1.3 0.8 %copy-start = (f32[13824]{0:T(1024)S(1)}, f32[13824]{0:T(1024)}, u32[]{:S(2)}) copy-start(f32[13824]{0:T(1024)} %param.13) | copy-start | bytes 165892
  2.1 0.8 %copy-start.1 = (s32[13824]{0:T(1024)S(1)}, s32[13824]{0:T(1024)}, u32[]{:S(2)}) copy-start(s32[13824]{0:T(1024)} %param.12) | copy-start | bytes 165892
  2.9 0.7 %copy-start.2 = (s32[4096]{0:T(1024)S(1)}, s32[4096]{0:T(1024)}, u32[]{:S(2)}) copy-start(s32[4096]{0:T(1024)} %param.10) | copy-start | bytes 49156
  3.6 0.7 %copy-start.3 = (s32[4096]{0:T(1024)S(1)}, s32[4096]{0:T(1024)}, u32[]{:S(2)}) copy-start(s32[4096]{0:T(1024)} %param.11) | copy-start | bytes 49156
  4.4 0.7 %copy-start.4 = (f32[8,128]{1,0:T(8,128)S(1)}, f32[8,128]{1,0:T(8,128)}, u32[]{:S(2)}) copy-start(f32[8,128]{1,0:T(8,128)} %cot_in.1) | copy-start | bytes 12292
  5.0 0.7 %copy-start.5 = (f32[128]{0:T(128)S(1)}, f32[128]{0:T(128)}, u32[]{:S(2)}) copy-start(f32[128]{0:T(128)} %param.16) | copy-start | bytes 1540

commit v4 on v3

--- a/solution.py
+++ b/solution.py
@@ -25,8 +25,12 @@
 
 
 TILE = 256
+HALVES = 2
 LAG = 3
-STEP = 1024
+STEP = 2048
+AHEAD = 2
+SPREAD_AT = 3
+MARGINS_AT = 6
 
 
 def tiles_of(total):
@@ -95,7 +99,10 @@
     bucket_count = corr.shape[0]
     net_count, paths = cot.shape
     rows = net_count * paths
-    own_rows = rows // groups
+    half_rows = rows // HALVES
+    half_nets = net_count // HALVES
+    own_rows = half_rows // groups
+    quarter = own_rows // 2
     tiles = tiles_of(bucket_count)
 
     entering = [
@@ -127,7 +134,7 @@
     table[...] = jnp.zeros_like(table)
     padded = hot.shape[0]
     if padded > bucket_count:
-        G[:, :, :, :, bucket_count:padded] = jnp.zeros(G.shape[:-1] + (padded - bucket_count,), BF16)
+        G[:, :, :, :, :, bucket_count:padded] = jnp.zeros(G.shape[:-1] + (padded - bucket_count,), BF16)
     for copy in entering:
         copy.wait()
     table_rows = rw.shape[0]
@@ -183,35 +190,39 @@
         at = t * TILE
         return pl.ds(at if isinstance(at, int) else pl.multiple_of(at, TILE), width)
 
-    def stage1(t, width):
-        cols = columns(t, width)
+    steps = len(tiles)
+    last = steps - 1
+    last_width = tiles[last][1]
+
+    def stage1(h, t, width):
+        cols, i = columns(t, width), h * steps + t
         for d in (2, 1, 3):
             kx, ky, in_row, in_column = mates(d)
-            yield remote(S.at[:, kx, 0, :, cols], recv1.at[0, d - 1, :, :, cols], 0, t, d, in_row)
-            yield remote(S.at[ky, :, 1, :, cols], recv1.at[1, d - 1, :, :, cols], 1, t, d, in_column)
-
-    def stage2(t, width):
-        cols = columns(t, width)
+            yield remote(S.at[h, :, kx, 0, :, cols], recv1.at[h, 0, d - 1, :, :, cols], 0, i, d, in_row)
+            yield remote(S.at[h, ky, :, 1, :, cols], recv1.at[h, 1, d - 1, :, :, cols], 1, i, d, in_column)
+
+    def stage2(h, t, width):
+        cols, i = columns(t, width), h * steps + t
         for d in (2, 1, 3):
             kx, ky, in_row, in_column = mates(d)
-            yield remote(st.at[0, ky, :, cols], recv2.at[0, d - 1, :, cols], 2, t, d, in_column)
-            yield remote(st.at[1, kx, :, cols], recv2.at[1, d - 1, :, cols], 3, t, d, in_row)
-
-    def gather1(t, width):
-        cols = columns(t, width)
-        own_a, own_b = G.at[y, x, 0, :, cols], G.at[y, x, 1, :, cols]
+            yield remote(st.at[h, 0, ky, :, cols], recv2.at[h, 0, d - 1, :, cols], 2, i, d, in_column)
+            yield remote(st.at[h, 1, kx, :, cols], recv2.at[h, 1, d - 1, :, cols], 3, i, d, in_row)
+
+    def gather1(h, t, width):
+        cols, i = columns(t, width), h * steps + t
+        own_a, own_b = G.at[h, y, x, 0, :, cols], G.at[h, y, x, 1, :, cols]
         for d in (2, 1, 3):
             kx, ky, in_row, in_column = mates(d)
-            yield remote(own_a, own_a, 4, t, d, in_column)
-            yield remote(own_b, own_b, 5, t, d, in_row)
-
-    def gather2(t, width):
-        cols = columns(t, width)
-        all_a, all_b = G.at[:, x, 0, :, cols], G.at[y, :, 1, :, cols]
+            yield remote(own_a, own_a, 4, i, d, in_column)
+            yield remote(own_b, own_b, 5, i, d, in_row)
+
+    def gather2(h, t, width):
+        cols, i = columns(t, width), h * steps + t
+        all_a, all_b = G.at[h, :, x, 0, :, cols], G.at[h, y, :, 1, :, cols]
         for d in (2, 1, 3):
             kx, ky, in_row, in_column = mates(d)
-            yield remote(all_a, all_a, 6, t, d, in_row)
-            yield remote(all_b, all_b, 7, t, d, in_column)
+            yield remote(all_a, all_a, 6, i, d, in_row)
+            yield remote(all_b, all_b, 7, i, d, in_column)
 
     def start(copies):
         for copy in copies:
@@ -221,92 +232,115 @@
         for copy in copies:
             copy.wait_recv()
 
-    def pass_on(t, width):
-        arrive(stage1(t, width))
+    def by_width(i, run):
+        h, t = i // steps, i % steps
+
+        @pl.when(t < last)
+        def _():
+            run(h, t, TILE)
+
+        @pl.when(t == last)
+        def _():
+            run(h, last, last_width)
+
+    def pass_on(h, t, width):
+        arrive(stage1(h, t, width))
         cols = columns(t, width)
-        total_a = S[:, x, 0, :, cols].astype(F32)
-        total_b = S[y, :, 1, :, cols].astype(F32)
+        total_a = S[h, :, x, 0, :, cols].astype(F32)
+        total_b = S[h, y, :, 1, :, cols].astype(F32)
         for d in range(OTHERS):
-            total_a += recv1[0, d, :, :, cols].astype(F32)
-            total_b += recv1[1, d, :, :, cols].astype(F32)
-        st[0, :, :, cols] = total_a.astype(BF16)
-        st[1, :, :, cols] = total_b.astype(BF16)
-        start(stage2(t, width))
-
-    last = len(tiles) - 1
-    last_width = tiles[last][1]
-
-    def forward(t, carry):
+            total_a += recv1[h, 0, d, :, :, cols].astype(F32)
+            total_b += recv1[h, 1, d, :, :, cols].astype(F32)
+        st[h, 0, :, :, cols] = total_a.astype(BF16)
+        st[h, 1, :, :, cols] = total_b.astype(BF16)
+        start(stage2(h, t, width))
+
+    def forward(i, carry):
+        h, t = i // steps, i % steps
         at = pl.multiple_of(t * TILE, TILE)
-        for i in range(capacity // CHUNK):
-            part = pl.ds(i * CHUNK, CHUNK)
-            bucket = wrow[:, part]
-            sub = (at + lax.broadcasted_iota(jnp.int32, (TILE, CHUNK), 0)).astype(F32)
-            hot[pl.ds(at, TILE), part] = jnp.where(sub == bucket, 1.0, 0.0).astype(BF16)
-        result = dot(X[...], hot[pl.ds(at, TILE), :], NT)
-        S[:, :, :, :, pl.ds(at, TILE)] = result.astype(BF16).reshape(S.shape[:-1] + (TILE,))
-
-        @pl.when(t == 0)
+
+        @pl.when(h == 0)
+        def _():
+            for k in range(capacity // CHUNK):
+                part = pl.ds(k * CHUNK, CHUNK)
+                bucket = wrow[:, part]
+                sub = (at + lax.broadcasted_iota(jnp.int32, (TILE, CHUNK), 0)).astype(F32)
+                hot[pl.ds(at, TILE), part] = jnp.where(sub == bucket, 1.0, 0.0).astype(BF16)
+
+        half = pl.ds(pl.multiple_of(h * half_rows, half_rows), half_rows)
+        result = dot(X[half, :], hot[pl.ds(at, TILE), :], NT).astype(BF16)
+        S[h, :, :, :, :, pl.ds(at, TILE)] = result.reshape(S.shape[1:-1] + (TILE,))
+
+        @pl.when(i == 0)
         def _():
             pl.semaphore_wait(barrier, groups - 1 + slabs - 1)
 
-        @pl.when(t < last)
-        def _():
-            start(stage1(t, TILE))
-
-        @pl.when(t == last)
-        def _():
-            start(stage1(last, last_width))
-
-        @pl.when(t >= LAG)
-        def _():
-            pass_on(t - LAG, TILE)
+        by_width(i, lambda h, t, width: start(stage1(h, t, width)))
+
+        @pl.when(i >= LAG)
+        def _():
+            by_width(i - LAG, pass_on)
 
         return carry
 
-    lax.fori_loop(0, len(tiles), forward, 0)
+    total_steps = HALVES * steps
+    lax.fori_loop(0, total_steps, forward, 0)
     c_copy.wait()
     for at, width in tiles:
         block = C[:, at : at + width]
         high = block.astype(BF16)
         Chi[:, at : at + width] = high
         Clo[:, at : at + width] = (block - high.astype(F32)).astype(BF16)
-    for t in range(len(tiles) - LAG, len(tiles)):
-        pass_on(t, tiles[t][1])
-    for t, (at, width) in enumerate(tiles):
-        arrive(stage2(t, width))
-        cols = pl.ds(at, width)
-        total_a = st[0, y, :, cols].astype(F32)
-        total_b = st[1, x, :, cols].astype(F32)
-        for d in range(OTHERS):
-            total_a += recv2[0, d, :, cols].astype(F32)
-            total_b += recv2[1, d, :, cols].astype(F32)
-        SF[0 : own_rows // 2, cols] = total_a
-        SF[own_rows // 2 : own_rows, cols] = total_b
-
-    summed = SF[...]
-    s_high = summed.astype(BF16)
-    s_low = (summed - s_high.astype(F32)).astype(BF16)
-    both = dot(jnp.concatenate([s_high, s_low], axis=0), Chi[...], NN)
-    coupled = both[0:own_rows] + both[own_rows:] + dot(s_high, Clo[...], NN)
-    margin = jnp.sqrt(jnp.sum(summed * coupled, axis=1, keepdims=True) + EPSILON)
+
     per_net = paths // own_rows
-    own_net, own_part = me // per_net, me % per_net
+    own_part = me % per_net
     sub = lax.broadcasted_iota(jnp.int32, (own_rows, paths), 0)
     lane = lax.broadcasted_iota(jnp.int32, (own_rows, paths), 1)
     mine = lane == sub + own_part * own_rows
     net_sub = lax.broadcasted_iota(jnp.int32, (net_count, paths), 0)
-    cot_row = jnp.sum(jnp.where(net_sub == own_net, cot[...], 0.0), axis=0, keepdims=True)
-    cot_column = jnp.sum(jnp.where(mine, cot_row, 0.0), axis=1, keepdims=True)
-    grad = ((cot_column / margin) * coupled).astype(BF16)
-    G[y, x, :, :, 0:bucket_count] = grad.reshape(2, own_rows // 2, bucket_count)
-
-    for t in reversed(range(len(tiles))):
-        start(gather1(t, tiles[t][1]))
-
-    margin_row = jnp.sum(jnp.where(mine, margin, 0.0), axis=0, keepdims=True)
-    my_margins = jnp.where(net_sub == own_net, margin_row, 0.0)
-    m_send[...] = my_margins
+
+    def own(h):
+        for t, (at, width) in enumerate(tiles):
+            arrive(stage2(h, t, width))
+            cols = pl.ds(at, width)
+            total_a = st[h, 0, y, :, cols].astype(F32)
+            total_b = st[h, 1, x, :, cols].astype(F32)
+            for d in range(OTHERS):
+                total_a += recv2[h, 0, d, :, cols].astype(F32)
+                total_b += recv2[h, 1, d, :, cols].astype(F32)
+            SF[0:quarter, cols] = total_a
+            SF[quarter:own_rows, cols] = total_b
+        summed = SF[...]
+        s_high = summed.astype(BF16)
+        s_low = (summed - s_high.astype(F32)).astype(BF16)
+        both = dot(jnp.concatenate([s_high, s_low], axis=0), Chi[...], NN)
+        coupled = both[0:own_rows] + both[own_rows:] + dot(s_high, Clo[...], NN)
+        margin = jnp.sqrt(jnp.sum(summed * coupled, axis=1, keepdims=True) + EPSILON)
+        own_net = h * half_nets + me // per_net
+        cot_row = jnp.sum(jnp.where(net_sub == own_net, cot[...], 0.0), axis=0, keepdims=True)
+        cot_column = jnp.sum(jnp.where(mine, cot_row, 0.0), axis=1, keepdims=True)
+        grad = ((cot_column / margin) * coupled).astype(BF16)
+        G[h, y, x, :, :, 0:bucket_count] = grad.reshape(2, quarter, bucket_count)
+        for t in reversed(range(steps)):
+            start(gather1(h, t, tiles[t][1]))
+        margin_row = jnp.sum(jnp.where(mine, margin, 0.0), axis=0, keepdims=True)
+        return jnp.where(net_sub == own_net, margin_row, 0.0)
+
+    def spread(h, chosen):
+        for t in chosen:
+            arrive(gather1(h, t, tiles[t][1]))
+            start(gather2(h, t, tiles[t][1]))
+
+    order = list(reversed(range(steps)))
+
+    early_margins = own(0)
+    for i in range(total_steps - LAG, total_steps):
+        h, t = i // steps, i % steps
+        pass_on(h, t, tiles[t][1])
+    spread(0, order[:AHEAD])
+    late_margins = own(1)
+    spread(0, order[AHEAD:])
+    m_send[...] = early_margins + late_margins
 
     def margin_copies():
         for d in range(1, groups):
@@ -319,11 +353,8 @@
                 device_id_type=MESH,
             )
 
-    for t in reversed(range(len(tiles))):
-        arrive(gather1(t, tiles[t][1]))
-        start(gather2(t, tiles[t][1]))
-        if t == last:
-            start(margin_copies())
+    start(margin_copies())
+
     def mean_copies():
         for d in range(1, slabs):
             yield pltpu.make_async_remote_copy(
@@ -346,38 +377,35 @@
         start(mean_copies())
 
     def backward(i, carry):
-        t = last - i
-
-        @pl.when(t < last)
-        def _():
-            arrive(gather2(t, TILE))
-
-        @pl.when(t == last)
-        def _():
-            arrive(gather2(last, last_width))
-
+        h, t = i // steps, last - i % steps
+
+        @pl.when(i == SPREAD_AT)
+        def _():
+            spread(1, order)
+
+        by_width(h * steps + t, lambda h, t, width: arrive(gather2(h, t, width)))
         at = pl.multiple_of(t * TILE, TILE)
 
         def one(i, carry):
             part = pl.ds(pl.multiple_of(i * STEP, STEP), STEP)
-            all_grad = G[:, :, :, :, pl.ds(at, TILE)].reshape(rows, TILE)
+            all_grad = G[h, :, :, :, :, pl.ds(at, TILE)].reshape(half_rows, TILE)
             looked_up = dot(all_grad, hot[pl.ds(at, TILE), part], NN)
             net = nets[:, part]
             total = acc[:, part]
-            for n in range(net_count):
-                total += jnp.where(net == n, looked_up[n * paths : (n + 1) * paths], 0.0)
+            for n in range(half_nets):
+                total += jnp.where(net == h * half_nets + n, looked_up[n * paths : (n + 1) * paths], 0.0)
             acc[:, part] = total
             return carry
 
         lax.fori_loop(0, capacity // STEP, one, carry, unroll=2)
 
-        @pl.when(i == 1)
+        @pl.when(i == MARGINS_AT)
         def _():
             margins()
 
         return carry
 
-    lax.fori_loop(0, len(tiles), backward, 0)
+    lax.fori_loop(0, total_steps, backward, 0)
     grad_o[...] = (acc[...] * weight[...]).astype(BF16)
 
     arrive(mean_copies())
@@ -386,10 +414,11 @@
         everyone += e_recv[d]
     expected_o[...] = everyone / (paths * slabs)
 
-    for t, (at, width) in enumerate(tiles):
-        for stage in (stage1, stage2, gather1, gather2):
-            for copy in stage(t, width):
-                copy.wait_send()
+    for h in range(HALVES):
+        for t, (at, width) in enumerate(tiles):
+            for stage in (stage1, stage2, gather1, gather2):
+                for copy in stage(h, t, width):
+                    copy.wait_send()
     for copy in (*margin_copies(), *mean_copies()):
         copy.wait_send()
 
@@ -411,13 +440,14 @@
     buckets = correlation.shape[0]
     net_count = margin_cotangent.shape[0]
     rows = net_count * paths
-    half = rows // groups // 2
+    half = rows // HALVES // groups // 2
     tile_count = len(tiles_of(buckets))
     padded = tile_count * TILE
     vmem = pl.BlockSpec(memory_space=pltpu.VMEM)
     smem = pl.BlockSpec(memory_space=pltpu.SMEM)
     dma = pltpu.SemaphoreType.DMA
-    anywhere = pl.BlockSpec(memory_space=pl.ANY)
+    anywhere = pl.BlockSpec(memory_space=pltpu.HBM)
+    in_hbm = functools.partial(pltpu.with_memory_space_constraint, memory_space=pltpu.HBM)
     margin, expected, turned_grad = pl.pallas_call(
         functools.partial(kernel, groups, slabs),
         out_shape=(
@@ -440,15 +470,15 @@
             pltpu.VMEM((padded, capacity), BF16),
             pltpu.VMEM((rows, capacity), BF16),
             pltpu.VMEM((1, capacity), F32),
-            pltpu.VMEM((SIDE, SIDE, 2, half, padded), BF16),
-            pltpu.VMEM((2, OTHERS, SIDE, half, buckets), BF16),
-            pltpu.VMEM((2, SIDE, half, buckets), BF16),
-            pltpu.VMEM((2, OTHERS, half, buckets), BF16),
+            pltpu.VMEM((HALVES, SIDE, SIDE, 2, half, padded), BF16),
+            pltpu.VMEM((HALVES, 2, OTHERS, SIDE, half, buckets), BF16),
+            pltpu.VMEM((HALVES, 2, SIDE, half, buckets), BF16),
+            pltpu.VMEM((HALVES, 2, OTHERS, half, buckets), BF16),
             pltpu.VMEM((2 * half, buckets), F32),
             pltpu.VMEM((buckets, buckets), F32),
             pltpu.VMEM((buckets, buckets), BF16),
             pltpu.VMEM((buckets, buckets), BF16),
-            pltpu.VMEM((SIDE, SIDE, 2, half, padded), BF16),
+            pltpu.VMEM((HALVES, SIDE, SIDE, 2, half, padded), BF16),
             pltpu.VMEM((paths, capacity), F32),
             pltpu.VMEM((net_count, paths), F32),
             pltpu.VMEM((groups - 1, net_count, paths), F32),
@@ -456,8 +486,8 @@
             pltpu.VMEM((slabs - 1, net_count, paths), F32),
             dma,
             dma((7,)),
-            dma((8, tile_count, OTHERS)),
-            dma((8, tile_count, OTHERS)),
+            dma((8, HALVES * tile_count, OTHERS)),
+            dma((8, HALVES * tile_count, OTHERS)),
             dma((groups - 1,)),
             dma((groups - 1,)),
             dma((slabs - 1,)),
@@ -468,15 +498,15 @@
         ),
         name="margin_exchange",
     )(
-        deltas,
-        net_ids.reshape(1, capacity),
-        block_ids.reshape(1, capacity),
-        risk_weight.reshape(-1, LANES),
-        bucket_map.reshape(-1, LANES),
+        in_hbm(deltas),
+        in_hbm(net_ids.reshape(1, capacity)),
+        in_hbm(block_ids.reshape(1, capacity)),
+        in_hbm(risk_weight.reshape(-1, LANES)),
+        in_hbm(bucket_map.reshape(-1, LANES)),
         counts,
-        correlation,
-        path_weight.reshape(1, paths),
-        margin_cotangent,
+        in_hbm(correlation),
+        in_hbm(path_weight.reshape(1, paths)),
+        in_hbm(margin_cotangent),
     )
     block = capacity // 2
     whole = pl.BlockSpec((net_count, paths), lambda i: (0, 0))

time: 63.3 us -> 61.3 us (0.968); the launches traced: 62.9 us -> 60.2 us
  local copies, waits for them, and re-layouts: 4.41 us -> 0 us
  Pallas kernels: 57.2 us -> 59 us
    unnamed x12 -> x0, local copies, waits for them, and re-layouts: 4.41 us -> none
    pallas_call x1, Pallas kernels: 56 us -> 57.7 us  [shards(): pl.pallas_call(functools.partial(kernel, groups, slabs), out_shape=(jax.S...]
where the time goes in v4:
time: 61.3 us; the launch traced here: 60.2 us
  Pallas kernels  59 us (96%)
  between operations  1.29 us (2%)
    pallas_call x1, Pallas kernels, shards(): pl.pallas_call(functools.partial(kernel, groups, slabs), out_shape=(jax.S...  57.7 us

profile of v4, /device:TPU:0, one launch (start us, length us, event | category | flops | bytes accessed | tf_op | source)
XLA Modules:
  0.0 60.2 jit_solution(11372250916965138605)
XLA Ops:
  1.3 57.7 %margin_exchange.1 = (f32[8,128]{1,0:T(8,128)S(1)}, f32[8,128]{1,0:T(8,128)S(1)}, bf16[128,4096]{1,0:T(8,128)(2,1)S(1)}) custom-call(bf16[4096,128]{1,0:T(8,128)(2,1)} %deltas_in.1, s32[1,4096]{1,0:T(1,128)} %bitcast.8, s32[1,4096]{1,0:T(1,128)} %bitcast.9, f32[108,128]{1,0:T(8,128)} %bitcast.6, s32[108,128]{1,0:T(8,128)} %bitcast.7, s32[1]{0:T(128)S(6)} %copy.12.counts, ...), custom_call_target="tpu_custom_call" | custom-call | tf_op jit(solution)/shard_map/margin_exchange/pallas_call | solution.py:451
  59.0 1.2 %finish.1 = (bf16[4096,128]{1,0:T(8,128)(2,1)}, f32[8,128]{1,0:T(8,128)}, f32[1,8]{1,0:T(1,128)}) custom-call(bf16[128,4096]{1,0:T(8,128)(2,1)S(1)} %get-tuple-element.9.grad, f32[8,128]{1,0:T(8,128)S(1)} %get-tuple-element.10.margin, f32[8,128]{1,0:T(8,128)S(1)} %get-tuple-element.11.expected), custom_call_target="tpu_custom_call" | custom-call | tf_op jit(solution)/shard_map/finish/pallas_call | solution.py:513

commit v5 on v4

--- a/solution.py
+++ b/solution.py
@@ -28,9 +28,9 @@
 HALVES = 2
 LAG = 3
 STEP = 2048
-AHEAD = 2
-SPREAD_AT = 3
-MARGINS_AT = 6
+AHEAD = 3
+SPREAD_AT = 2
+MARGINS_AT = 5
 
 
 def tiles_of(total):
@@ -122,7 +122,6 @@
     for copy in entering:
         copy.start()
     c_copy = pltpu.make_async_copy(corr, C, c_sem)
-    c_copy.start()
 
     barrier = pltpu.get_barrier_semaphore()
     for d in range(1, groups):
@@ -130,13 +129,10 @@
     for d in range(1, slabs):
         pl.semaphore_signal(barrier, inc=1, device_id={"path": (slab + d) % slabs}, device_id_type=MESH)
 
-    acc[...] = jnp.zeros_like(acc)
     table[...] = jnp.zeros_like(table)
-    padded = hot.shape[0]
-    if padded > bucket_count:
-        G[:, :, :, :, :, bucket_count:padded] = jnp.zeros(G.shape[:-1] + (padded - bucket_count,), BF16)
     for copy in entering:
         copy.wait()
+    c_copy.start()
     table_rows = rw.shape[0]
     w_all = rw[...]
     w1 = w_all.astype(BF16).astype(F32)
@@ -163,11 +159,10 @@
         weight[:, pl.ds(at, CHUNK)] = w
         wrow[:, pl.ds(at, CHUNK)] = parts[2] * LANES + parts[3]
         turned = slots[pl.ds(at, CHUNK), :].T.astype(F32)
-        weighted = (turned * w).astype(BF16)
+        weighted = turned * w
         net = nets[:, pl.ds(at, CHUNK)]
         for n in range(net_count):
-            mask = jnp.where(net == n, 1.0, 0.0).astype(BF16)
-            X[n * paths : (n + 1) * paths, pl.ds(at, CHUNK)] = weighted * mask
+            X[n * paths : (n + 1) * paths, pl.ds(at, CHUNK)] = jnp.where(net == n, weighted, 0.0).astype(BF16)
         return carry
 
     lax.fori_loop(0, capacity // CHUNK, look_up, 0, unroll=4)
@@ -334,6 +329,10 @@
     order = list(reversed(range(steps)))
 
     early_margins = own(0)
+    acc[...] = jnp.zeros_like(acc)
+    padded = hot.shape[0]
+    if padded > bucket_count:
+        G[:, :, :, :, :, bucket_count:padded] = jnp.zeros(G.shape[:-1] + (padded - bucket_count,), BF16)
     for i in range(total_steps - LAG, total_steps):
         h, t = i // steps, i % steps
         pass_on(h, t, tiles[t][1])

time: 61.3 us -> 58.3 us (0.951)
  Pallas kernels: 59 us -> 56 us
    pallas_call x1, Pallas kernels: 57.7 us -> 54.8 us  [shards(): pl.pallas_call(functools.partial(kernel, groups, slabs), out_shape=(jax.S...]
where the time goes in v5:
time: 58.3 us; the launch traced here: 57.3 us
  Pallas kernels  56 us (96%)
  between operations  1.29 us (2%)
    pallas_call x1, Pallas kernels, shards(): pl.pallas_call(functools.partial(kernel, groups, slabs), out_shape=(jax.S...  54.8 us
    pallas_call x1, Pallas kernels, shards(): pl.pallas_call(finish, grid=(capacity // block,), out_shape=(jax.ShapeDty...  1.21 us

profile of v5, /device:TPU:0, one launch (start us, length us, event | category | flops | bytes accessed | tf_op | source)
XLA Modules:
  0.0 57.3 jit_solution(10277909986830128839)
XLA Ops:
  1.3 54.8 %margin_exchange.1 = (f32[8,128]{1,0:T(8,128)S(1)}, f32[8,128]{1,0:T(8,128)S(1)}, bf16[128,4096]{1,0:T(8,128)(2,1)S(1)}) custom-call(bf16[4096,128]{1,0:T(8,128)(2,1)} %deltas_in.1, s32[1,4096]{1,0:T(1,128)} %bitcast.8, s32[1,4096]{1,0:T(1,128)} %bitcast.9, f32[108,128]{1,0:T(8,128)} %bitcast.6, s32[108,128]{1,0:T(8,128)} %bitcast.7, s32[1]{0:T(128)S(6)} %copy.12.counts, ...), custom_call_target="tpu_custom_call" | custom-call | tf_op jit(solution)/shard_map/margin_exchange/pallas_call | solution.py:450
  56.0 1.2 %finish.1 = (bf16[4096,128]{1,0:T(8,128)(2,1)}, f32[8,128]{1,0:T(8,128)}, f32[1,8]{1,0:T(1,128)}) custom-call(bf16[128,4096]{1,0:T(8,128)(2,1)S(1)} %get-tuple-element.9.grad, f32[8,128]{1,0:T(8,128)S(1)} %get-tuple-element.10.margin, f32[8,128]{1,0:T(8,128)S(1)} %get-tuple-element.11.expected), custom_call_target="tpu_custom_call" | custom-call | tf_op jit(solution)/shard_map/finish/pallas_call | solution.py:512

commit v6 on v5

--- a/solution.py
+++ b/solution.py
@@ -148,10 +148,11 @@
         high, low = ids // LANES, ids % LANES
         sub = lax.broadcasted_iota(jnp.int32, (LANES, CHUNK), 0)
         pick = jnp.where(sub == high, 1.0, 0.0).astype(BF16)
-        found = dot(table[...], pick, NN)
         keep = sub == low
         parts = [
-            jnp.sum(jnp.where(keep, found[k * LANES : (k + 1) * LANES], 0.0), axis=0, keepdims=True)
+            jnp.sum(
+                jnp.where(keep, dot(table[k * LANES : (k + 1) * LANES], pick, NN), 0.0), axis=0, keepdims=True
+            )
             for k in range(4)
         ]
         slot = at + lax.broadcasted_iota(jnp.int32, (1, CHUNK), 1)

time: 58.3 us -> 58.5 us (level)
  no operation moved by 1% of the time
where the time goes in v6:
time: 58.5 us; the launch traced here: 57.4 us
  Pallas kernels  56.1 us (96%)
  between operations  1.29 us (2%)
    pallas_call x1, Pallas kernels, shards(): pl.pallas_call(functools.partial(kernel, groups, slabs), out_shape=(jax.S...  54.9 us
    pallas_call x1, Pallas kernels, shards(): pl.pallas_call(finish, grid=(capacity // block,), out_shape=(jax.ShapeDty...  1.21 us

profile of v6, /device:TPU:0, one launch (start us, length us, event | category | flops | bytes accessed | tf_op | source)
XLA Modules:
  0.0 57.4 jit_solution(4116882207051374293)
XLA Ops:
  1.3 54.9 %margin_exchange.1 = (f32[8,128]{1,0:T(8,128)S(1)}, f32[8,128]{1,0:T(8,128)S(1)}, bf16[128,4096]{1,0:T(8,128)(2,1)S(1)}) custom-call(bf16[4096,128]{1,0:T(8,128)(2,1)} %deltas_in.1, s32[1,4096]{1,0:T(1,128)} %bitcast.8, s32[1,4096]{1,0:T(1,128)} %bitcast.9, f32[108,128]{1,0:T(8,128)} %bitcast.6, s32[108,128]{1,0:T(8,128)} %bitcast.7, s32[1]{0:T(128)S(6)} %copy.12.counts, ...), custom_call_target="tpu_custom_call" | custom-call | tf_op jit(solution)/shard_map/margin_exchange/pallas_call | solution.py:451
  56.2 1.2 %finish.1 = (bf16[4096,128]{1,0:T(8,128)(2,1)}, f32[8,128]{1,0:T(8,128)}, f32[1,8]{1,0:T(1,128)}) custom-call(bf16[128,4096]{1,0:T(8,128)(2,1)S(1)} %get-tuple-element.9.grad, f32[8,128]{1,0:T(8,128)S(1)} %get-tuple-element.10.margin, f32[8,128]{1,0:T(8,128)S(1)} %get-tuple-element.11.expected), custom_call_target="tpu_custom_call" | custom-call | tf_op jit(solution)/shard_map/finish/pallas_call | solution.py:513
